TPU v7x, 32 devices: a whole 2x2x4 slice. The times are simulated.
32 devices in a mesh: dp: 8 (over z, y), tp: 4 (over x, core).
Axes of the slice: x: 2, y: 2, z: 4, core: 2. Of those that a mesh axis runs over, the one named last changes fastest.
Arguments:
- tokens: bfloat16 [768, 2880], P('dp', 'tp'), may hold values from -100 to 100
- attn_gain: float32 [2880], replicated, may hold values from 0.1 to 1.9
- w_query: bfloat16 [2880, 2048], P(None, 'tp'), may hold values from -0.109375 to 0.109375
- w_keyvalue: bfloat16 [2880, 8, 128], P(None, 'tp'), may hold values from -0.109375 to 0.109375
- attn_sinks: float32 [32], P('tp'), may hold values from 2 to 6
- w_out: bfloat16 [2048, 2880], P('tp'), may hold values from -0.125 to 0.125
- window_cache: bfloat16 [768, 8, 128, 128], P('dp', 'tp'), may hold values from -1000 to 1000
- positions: int32 [768], P('dp'), may hold values from 0 to 511
- moe_gain: float32 [2880], replicated, may hold values from 0.1 to 1.9
- router: bfloat16 [2880, 8], P('tp'), may hold values from -0.109375 to 0.109375
- gate_up: bfloat16 [8, 2880, 2, 2880], P('dp', None, None, 'tp'), may hold values from -0.109375 to 0.109375
- w_down: bfloat16 [8, 2880, 2880], P('dp', None, 'tp'), may hold values from -0.109375 to 0.109375
- expert_ids: int32 [768, 4], P('dp'), may hold values from 0 to 7, all different within a row; in each aligned block of 96 rows (0 to 95, 96 to 191, ...) at most 96 rows name the same one
Outputs:
- layer_out: float32 [768, 2880], P('dp', 'tp')
Inputs may be any that keep to these rules, and one draw needn't show every extreme that they name: `expert_ids`: each row names 4 different experts. Within the rows of one index of dp no expert is named by more than 96 rows, a bound that some of these blocks reach.
All inputs are finite; a program needn't handle non-finite values.
Results may differ from a plain program's by a relative error of at most 0.0066.
Values may be sent and summed in bfloat16 or wider, within the bound.
A program may use at most 128 MiB of HBM per device.

v0:
```python
import functools
import math

import jax
import jax.numpy as jnp
from jax import lax
from jax.experimental import pallas as pl
from jax.experimental.pallas import tpu as pltpu
from jax.sharding import PartitionSpec as P

norm_eps = 1e-05
rope_base = 150000.0
glu_alpha = 1.702


def rope_tables(positions, head_size):
    half_size = head_size // 2
    exponent = jnp.arange(half_size, dtype=jnp.float32) * (2.0 / head_size)
    inverse = jnp.power(jnp.float32(rope_base), -exponent)
    angles = positions.astype(jnp.float32)[:, None] * inverse[None, :]
    return (jnp.cos(angles), jnp.sin(angles))


def rotate(values, cosine, sine_table):
    half_size = values.shape[-1] // 2
    first_half = values[..., :half_size]
    second_half = values[..., half_size:]
    return jnp.concatenate(
        [
            first_half * cosine - second_half * sine_table,
            second_half * cosine + first_half * sine_table,
        ],
        axis=-1,
    )


MESH = pl.DeviceIdType.MESH
CORES = 2


def greet(partners):
    barrier = pltpu.get_barrier_semaphore()
    for partner in partners:
        pl.semaphore_signal(barrier, inc=1, device_id=partner, device_id_type=MESH)
    pl.semaphore_wait(barrier, len(partners))


def feature_gather_kernel(tp, chunks, x_ref, out_ref, buf, own_sem, send_x, send_c, recv):
    chips = tp // CORES
    dp_id = lax.axis_index("dp")
    me = lax.axis_index("tp")
    core = lax.rem(me, CORES)
    chip = me // CORES
    rows, cols = x_ref.shape
    step = rows // chunks
    twin = (dp_id, chip * CORES + (1 - core))
    others = [lax.rem(chip + d, chips) * CORES + core for d in range(1, chips)]
    sources = [lax.rem(chip + chips - d, chips) * CORES + core for d in range(1, chips)]
    own = pltpu.make_async_copy(x_ref, buf.at[me], own_sem)
    own.start()
    greet([twin] + [(dp_id, other) for other in others])

    def piece(k):
        return pl.ds(k * step, step)

    def send(src, origin, k, sem, target):
        return pltpu.make_async_remote_copy(
            src_ref=src, dst_ref=buf.at[origin, piece(k)], send_sem=sem,
            recv_sem=recv.at[origin, k], device_id=target, device_id_type=MESH)

    sent = []
    for k in range(chunks):
        for d in range(chips - 1):
            sent.append(send(x_ref.at[piece(k)], me, k, send_x.at[d, k], (dp_id, others[d])))
            sent[-1].start()
    for k in range(chunks):
        sent.append(send(x_ref.at[piece(k)], me, k, send_c.at[0, k], twin))
        sent[-1].start()
    own.wait()
    for k in range(chunks):
        for d in range(chips - 1):
            origin = sources[d]
            forward = send(buf.at[origin, piece(k)], origin, k, send_c.at[d + 1, k], twin)
            forward.wait_recv()
            forward.start()
            sent.append(forward)
        if k:
            finish(tp, k - 1, step, chip, core, chips, buf, recv, out_ref, send, twin)
    finish(tp, chunks - 1, step, chip, core, chips, buf, recv, out_ref, send, twin)
    for copy in sent:
        copy.wait_send()


def finish(tp, k, step, chip, core, chips, buf, recv, out_ref, send, twin):
    cols = buf.shape[2]
    part = pl.ds(k * step, step)
    for d in range(chips):
        origin = lax.rem(chip + d, chips) * CORES + (1 - core)
        pltpu.make_async_remote_copy(
            src_ref=buf.at[origin, part], dst_ref=buf.at[origin, part], send_sem=recv.at[origin, k],
            recv_sem=recv.at[origin, k], device_id=twin, device_id_type=MESH).wait_recv()
    for t in range(tp):
        out_ref[part, t * cols:(t + 1) * cols] = buf[t, part, :]


def feature_gather(x, tp, chunks, collective_id):
    rows, cols = x.shape
    chips = tp // CORES
    return pl.pallas_call(
        functools.partial(feature_gather_kernel, tp, chunks),
        out_shape=jax.ShapeDtypeStruct((rows, tp * cols), x.dtype),
        in_specs=[pl.BlockSpec(memory_space=pltpu.VMEM)],
        out_specs=pl.BlockSpec(memory_space=pltpu.VMEM),
        scratch_shapes=[
            pltpu.VMEM((tp, rows, cols), x.dtype),
            pltpu.SemaphoreType.DMA,
            pltpu.SemaphoreType.DMA((max(chips - 1, 1), chunks)),
            pltpu.SemaphoreType.DMA((chips, chunks)),
            pltpu.SemaphoreType.DMA((tp, chunks)),
        ],
        compiler_params=pltpu.CompilerParams(
            collective_id=collective_id, has_side_effects=True, vmem_limit_bytes=48 * 2**20),
        cost_estimate=pl.CostEstimate(flops=0, bytes_accessed=rows * cols * tp * 16, transcendentals=0),
    )(x)


def share_sum_kernel(tp, scatter, x_ref, out_ref, buf, send_sem, recv_sem):
    chips = tp // CORES
    dp_id = lax.axis_index("dp")
    me = lax.axis_index("tp")
    core = lax.rem(me, CORES)
    chip = me // CORES
    others = [
        lax.rem(chip + d, chips) * CORES + c for d in range(1, chips) for c in range(CORES)
    ] + [chip * CORES + (1 - core)]
    greet([(dp_id, other) for other in others])
    sent = []
    for i, other in enumerate(others):
        sent.append(pltpu.make_async_remote_copy(
            src_ref=x_ref.at[other if scatter else 0], dst_ref=buf.at[me], send_sem=send_sem.at[i],
            recv_sem=recv_sem.at[me], device_id=(dp_id, other), device_id_type=MESH))
        sent[-1].start()
    total = x_ref[me if scatter else 0].astype(jnp.float32)
    for i in reversed(range(len(others))):
        other = others[i]
        pltpu.make_async_remote_copy(
            src_ref=buf.at[other], dst_ref=buf.at[other], send_sem=send_sem.at[i],
            recv_sem=recv_sem.at[other], device_id=(dp_id, other), device_id_type=MESH).wait_recv()
        total = total + buf[other].astype(jnp.float32)
    out_ref[...] = total
    for copy in sent:
        copy.wait_send()


def share_sum(x, tp, scatter, collective_id):
    rows, cols = x.shape[1:]
    return pl.pallas_call(
        functools.partial(share_sum_kernel, tp, scatter),
        out_shape=jax.ShapeDtypeStruct((rows, cols), jnp.float32),
        in_specs=[pl.BlockSpec(memory_space=pltpu.VMEM)],
        out_specs=pl.BlockSpec(memory_space=pltpu.VMEM),
        scratch_shapes=[
            pltpu.VMEM((tp, rows, cols), x.dtype),
            pltpu.SemaphoreType.DMA((tp - 1,)),
            pltpu.SemaphoreType.DMA((tp,)),
        ],
        compiler_params=pltpu.CompilerParams(
            collective_id=collective_id, has_side_effects=True, vmem_limit_bytes=16 * 2**20),
        cost_estimate=pl.CostEstimate(flops=0, bytes_accessed=rows * cols * tp * 16, transcendentals=0),
    )(x)


def full_gather_kernel(dp, ny, tp, x_ref, out_ref, buf, own_sem, send_z, send_x, send_y, send_c, recv):
    nz, nx = dp // ny, tp // CORES
    dp_id = lax.axis_index("dp")
    me = lax.axis_index("tp")
    core, x = lax.rem(me, CORES), me // CORES
    z, y = dp_id // ny, lax.rem(dp_id, ny)
    rows, cols = x_ref.shape
    half = rows // 2

    def place(pz, py, px, pc=core):
        return (pz * ny + py, px * CORES + pc)

    def around(v, d, n):
        return lax.rem(v + d, n)

    own = pltpu.make_async_copy(x_ref, buf.at[dp_id, me], own_sem)
    own.start()
    twin = place(z, y, x, 1 - core)
    x_others = [place(z, y, around(x, d, nx)) for d in range(1, nx)]
    y_others = [place(z, around(y, d, ny), x) for d in range(1, ny)]
    ring = [place(lax.rem(z + d, nz), y, x) for d in sorted({1 % nz, nz - 1} - {0})]
    greet([twin] + x_others + y_others + ring)
    own.wait()

    def copy(origin, h, sem, target):
        view = buf.at[origin[0], origin[1], pl.ds(h * half, half)]
        return pltpu.make_async_remote_copy(
            src_ref=view, dst_ref=view, send_sem=sem.at[origin[0], origin[1] // CORES, h],
            recv_sem=recv.at[origin[0], origin[1], h], device_id=target, device_id_type=MESH)

    def arrived(origin, h):
        view = buf.at[origin[0], origin[1], pl.ds(h * half, half)]
        pltpu.make_async_remote_copy(
            src_ref=view, dst_ref=view, send_sem=recv.at[origin[0], origin[1], h],
            recv_sem=recv.at[origin[0], origin[1], h], device_id=twin, device_id_type=MESH).wait_recv()

    def to_x(origin, h, act):
        for d in range(nx - 1):
            act(copy(origin, h, send_x.at[d], x_others[d]))

    def to_y(origin, h, act):
        for d in range(ny - 1):
            act(copy(origin, h, send_y.at[d], y_others[d]))

    def to_twin(origin, h, act):
        act(copy(origin, h, send_c, twin))

    def start(c):
        c.start()

    def ended(c):
        c.wait_send()

    def spread(origin, act):
        to_x(origin, 0, act)
        to_y(origin, 1, act)
        to_y(origin, 0, act)
        to_x(origin, 1, act)
        for h in range(2):
            to_twin(origin, h, act)

    def sideways(pz, act, wait):
        for d in range(1, nx):
            origin = place(pz, y, around(x, d, nx))
            if wait:
                arrived(origin, 0)
            to_y(origin, 0, act)
            to_twin(origin, 0, act)
        for d in range(1, ny):
            origin = place(pz, around(y, d, ny), x)
            if wait:
                arrived(origin, 1)
            to_x(origin, 1, act)
            to_twin(origin, 1, act)

    def last(pz, act, wait):
        for d in range(1, ny):
            for e in range(nx):
                origin = place(pz, around(y, d, ny), around(x, e, nx))
                if wait:
                    arrived(origin, 0)
                to_twin(origin, 0, act)
        for d in range(1, nx):
            for e in range(ny):
                origin = place(pz, around(y, e, ny), around(x, d, nx))
                if wait:
                    arrived(origin, 1)
                to_twin(origin, 1, act)

    def above(pz, act):
        @pl.when(z > 0)
        def _():
            for h in range(2):
                act(copy(place(pz, y, x), h, send_z.at[0], place(z - 1, y, x)))

    def below(pz, act):
        @pl.when(z < nz - 1)
        def _():
            for h in range(2):
                act(copy(place(pz, y, x), h, send_z.at[1], place(z + 1, y, x)))

    mine = place(z, y, x)
    above(z, start)
    below(z, start)
    spread(mine, start)

    def first_wave(pz, onward):
        origin = place(pz, y, x)
        arrived(origin, 0)
        arrived(origin, 1)
        onward(pz, start)
        spread(origin, start)

    sideways(z, start, True)
    for s in range(1, nz):
        for pz, ok, onward in ((z - s, z - s >= 0, below), (z + s, z + s < nz, above)):
            pl.when(ok)(functools.partial(first_wave, pz, onward))
        for pz, ok in ((z - s, z - s >= 0), (z + s, z + s < nz)):
            pl.when(ok)(functools.partial(sideways, pz, start, True))
        if s == 1:
            last(z, start, True)
        else:
            for pz, ok in ((z - s + 1, z - s + 1 >= 0), (z + s - 1, z + s - 1 < nz)):
                pl.when(ok)(functools.partial(last, pz, start, True))
    for pz, ok in ((z - nz + 1, z - nz + 1 >= 0), (z + nz - 1, z + nz - 1 < nz)):
        pl.when(ok)(functools.partial(last, pz, start, True))

    for b in range(dp):
        for px in range(nx):
            for h in range(2):
                arrived((b, px * CORES + 1 - core), h)
        for h in range(2):
            start_row = (h * dp + b) * half
            for t in range(tp):
                out_ref[start_row:start_row + half, t * cols:(t + 1) * cols] = buf[
                    b, t, h * half:(h + 1) * half
                ]

    def ends(pz, onward=None):
        if onward is not None:
            onward(pz, ended)
        spread(place(pz, y, x), ended)
        sideways(pz, ended, False)
        last(pz, ended, False)

    above(z, ended)
    below(z, ended)
    ends(z)
    for s in range(1, nz):
        for pz, ok, onward in ((z - s, z - s >= 0, below), (z + s, z + s < nz, above)):
            pl.when(ok)(functools.partial(ends, pz, onward))


def full_gather(x, dp, tp, collective_id):
    rows, cols = x.shape
    nx = tp // CORES
    ny = 2 ** (int(math.log2(dp)) // 2)
    per_piece = (dp, nx, 2)
    return pl.pallas_call(
        functools.partial(full_gather_kernel, dp, ny, tp),
        out_shape=jax.ShapeDtypeStruct((dp * rows, tp * cols), x.dtype),
        in_specs=[pl.BlockSpec(memory_space=pltpu.VMEM)],
        out_specs=pl.BlockSpec(memory_space=pltpu.VMEM),
        scratch_shapes=[
            pltpu.VMEM((dp, tp, rows, cols), x.dtype),
            pltpu.SemaphoreType.DMA,
            pltpu.SemaphoreType.DMA((2,) + per_piece),
            pltpu.SemaphoreType.DMA((max(nx - 1, 1),) + per_piece),
            pltpu.SemaphoreType.DMA((max(ny - 1, 1),) + per_piece),
            pltpu.SemaphoreType.DMA(per_piece),
            pltpu.SemaphoreType.DMA((dp, tp, 2)),
        ],
        compiler_params=pltpu.CompilerParams(
            collective_id=collective_id, has_side_effects=True, vmem_limit_bytes=48 * 2**20),
        cost_estimate=pl.CostEstimate(flops=0, bytes_accessed=rows * cols * dp * tp * 8, transcendentals=0),
    )(x)


def activate(mixed_in, ff_local):
    gate_part = mixed_in[..., :ff_local]
    up_part = mixed_in[..., ff_local:]
    return (gate_part * jax.nn.sigmoid(glu_alpha * gate_part) * (up_part + 1.0)).astype(
        jnp.bfloat16
    )


def on_device(
    tokens,
    attn_gain,
    w_query,
    w_keyvalue,
    attn_sinks,
    w_out,
    window_cache,
    positions,
    moe_gain,
    router,
    gate_up,
    w_down,
    expert_ids,
):
    tp_count = lax.axis_size("tp")
    dp_count = lax.axis_size("dp")
    seq_count, col_count = tokens.shape
    full_width = col_count * tp_count
    col_start = lax.axis_index("tp") * col_count
    head_size = w_keyvalue.shape[2] // 2
    kv_local = w_keyvalue.shape[1]
    q_local = w_query.shape[1] // head_size
    group_size = q_local // kv_local
    window = window_cache.shape[2]
    moe_slice = lax.dynamic_slice_in_dim(moe_gain, col_start, col_count)
    tok_wide = tokens.astype(jnp.float32)
    kv_flat = w_keyvalue.reshape(full_width, kv_local * 2 * head_size)
    whole_rows = feature_gather(tokens, tp_count, 2, 0).astype(jnp.float32)
    attn_sq = jnp.sum(whole_rows * whole_rows, axis=1, keepdims=True)
    piece_rows = (
        whole_rows * lax.rsqrt(attn_sq / full_width + norm_eps) * attn_gain[None, :]
    ).astype(jnp.bfloat16)
    queries = jnp.dot(piece_rows, w_query, preferred_element_type=jnp.float32)
    fresh_rows = jnp.dot(piece_rows, kv_flat, preferred_element_type=jnp.float32)
    cosine, sine_table = rope_tables(positions, head_size)
    rot_queries = rotate(
        queries.reshape(seq_count, q_local, head_size), cosine[:, None, :], sine_table[:, None, :]
    ).astype(jnp.bfloat16)
    fresh_rows = fresh_rows.reshape(seq_count, kv_local, 2 * head_size)
    new_key = rotate(fresh_rows[..., :head_size], cosine[:, None, :], sine_table[:, None, :])
    new_entry = jnp.concatenate([new_key, fresh_rows[..., head_size:]], axis=-1).astype(
        jnp.bfloat16
    )
    slot_ids = jnp.arange(window, dtype=jnp.int32)
    is_current = slot_ids[None, :] == (positions % window)[:, None]
    is_valid = (positions[:, None] - slot_ids[None, :]) % window <= positions[:, None]
    is_valid = is_valid & ~is_current
    grouped = rot_queries.reshape(seq_count, kv_local, group_size, head_size)
    scores = jnp.einsum(
        "skgh,skwh->skgw", grouped, window_cache[..., :head_size], preferred_element_type=jnp.float32
    ) * head_size ** (-0.5)
    scores = jnp.where(is_valid[:, None, None, :], scores, -jnp.inf)
    new_wide = new_entry.astype(jnp.float32)[:, :, None, :]
    new_score = jnp.sum(
        grouped.astype(jnp.float32) * new_wide[..., :head_size], axis=-1, keepdims=True
    ) * head_size ** (-0.5)
    sink_col = attn_sinks.reshape(kv_local, group_size)[None, :, :, None]
    peak_score = jnp.maximum(
        jnp.maximum(jnp.max(scores, axis=-1, keepdims=True), new_score), sink_col
    )
    raised = jnp.exp(scores - peak_score)
    raised_new = jnp.exp(new_score - peak_score)
    denominator = (
        jnp.sum(raised, axis=-1, keepdims=True) + raised_new + jnp.exp(sink_col - peak_score)
    )
    prob_bf = (raised / denominator).astype(jnp.bfloat16)
    prob_new = (raised_new / denominator).astype(jnp.bfloat16).astype(jnp.float32)
    attended = jnp.einsum(
        "skgw,skwh->skgh", prob_bf, window_cache[..., head_size:], preferred_element_type=jnp.float32
    )
    attended = (attended + prob_new * new_wide[..., head_size:]).astype(jnp.bfloat16)
    partial_out = jnp.einsum(
        "sh,htc->tsc",
        attended.reshape(seq_count, q_local * head_size),
        w_out.reshape(q_local * head_size, tp_count, col_count),
        preferred_element_type=jnp.float32,
    ).astype(jnp.bfloat16)
    residual = tok_wide + share_sum(partial_out, tp_count, True, 2)
    experts = router.shape[1]
    top_count = expert_ids.shape[1]
    local_experts = gate_up.shape[0]
    ff_local = gate_up.shape[3]
    capacity = min(seq_count, max(2, 8 * seq_count * top_count // (3 * experts)))
    moe_sq = jnp.sum(residual * residual, axis=1)
    router_wide = router.astype(jnp.float32)
    gained = residual * moe_slice[None, :]
    raw_logits = jnp.dot(gained, router_wide, precision=lax.Precision.HIGHEST)
    stats = share_sum(
        jnp.concatenate([moe_sq[:, None], raw_logits], axis=1)[None], tp_count, False, 3
    )
    moe_scale = lax.rsqrt(stats[:, :1] / full_width + norm_eps)
    logits = stats[:, 1:] * moe_scale
    hidden_rows = (gained * moe_scale).astype(jnp.bfloat16)
    expert_iota = jnp.arange(experts, dtype=jnp.int32)
    chosen = expert_ids[:, :, None] == expert_iota[None, None, :]
    picked = jnp.sum(jnp.where(chosen, logits[:, None, :], 0.0), axis=-1)
    raised_logits = jnp.exp(picked)
    route_weights = raised_logits / jnp.sum(raised_logits, axis=1, keepdims=True)
    gate_up_flat = gate_up.reshape(local_experts, full_width, 2 * ff_local)
    if capacity >= seq_count:
        token_weights = jnp.sum(jnp.where(chosen, route_weights[:, :, None], 0.0), axis=1)
        all_rows = full_gather(hidden_rows, dp_count, tp_count, 1)
        half = seq_count // 2
        part = dp_count * half
        acts = [
            activate(
                jnp.dot(all_rows, gate_up_flat[e], preferred_element_type=jnp.float32), ff_local
            )
            for e in range(local_experts)
        ]
        pieces = []
        for h in range(2):
            outs = []
            for e in range(local_experts):
                act_all = feature_gather(
                    acts[e][h * part : (h + 1) * part], tp_count, dp_count // 2, 4 + 2 * e + h
                )
                out = jnp.dot(act_all, w_down[e], preferred_element_type=jnp.float32)
                outs.append(out.astype(jnp.bfloat16).reshape(dp_count, half, col_count))
            returned = lax.all_to_all(
                jnp.stack(outs, axis=1), "dp", split_axis=0, concat_axis=0, tiled=True
            )
            back = returned.reshape(experts, half, col_count)
            mine = slice(h * half, (h + 1) * half)
            total = residual[mine]
            for e in range(experts):
                total = total + token_weights[mine, e : e + 1] * back[e].astype(jnp.float32)
            pieces.append(total)
        total = jnp.concatenate(pieces, axis=0)
        return total
    assign = expert_ids.reshape(-1)
    onehot = (assign[:, None] == expert_iota[None, :]).astype(jnp.int32)
    earlier = jnp.cumsum(onehot, axis=0) - onehot
    slot_of = jnp.sum(earlier * onehot, axis=1)
    target = (assign * capacity + slot_of).reshape(seq_count, top_count)
    spot_ids = jnp.arange(experts * capacity, dtype=jnp.int32)
    slot_hits = target[:, :, None] == spot_ids[None, None, :]
    placer = jnp.transpose(jnp.any(slot_hits, axis=1)).astype(jnp.bfloat16)
    combiner = jnp.sum(jnp.where(slot_hits, route_weights[:, :, None], 0.0), axis=1)
    placed = jnp.dot(placer, hidden_rows, preferred_element_type=jnp.float32).astype(jnp.bfloat16)
    mixed_in = jnp.einsum(
        "gecd,edf->gecf",
        lax.all_gather(
            lax.all_to_all(
                placed.reshape(dp_count, local_experts, capacity, hidden_rows.shape[1]),
                "dp",
                split_axis=0,
                concat_axis=0,
                tiled=True,
            ),
            "tp",
            axis=3,
            tiled=True,
        ),
        gate_up_flat,
        preferred_element_type=jnp.float32,
    )
    act_rows = activate(mixed_in, ff_local)
    answered = jnp.einsum(
        "gecf,efd->gecd",
        lax.all_gather(act_rows, "tp", axis=3, tiled=True),
        w_down,
        preferred_element_type=jnp.float32,
    ).astype(jnp.bfloat16)
    returned = lax.all_to_all(answered, "dp", split_axis=0, concat_axis=0, tiled=True)
    flat_back = returned.reshape(experts * capacity, col_count).astype(jnp.float32)
    moe_out = jnp.dot(combiner, flat_back, precision=lax.Precision.HIGHEST)
    return residual + moe_out


def solution(mesh):
    in_specs = (
        P("dp", "tp"),
        P(),
        P(None, "tp"),
        P(None, "tp", None),
        P("tp"),
        P("tp", None),
        P("dp", "tp", None, None),
        P("dp"),
        P(),
        P("tp", None),
        P("dp", None, None, "tp"),
        P("dp", None, "tp"),
        P("dp", None),
    )
    out_specs = P("dp", "tp")
    return jax.shard_map(
        on_device, mesh=mesh, in_specs=in_specs, out_specs=out_specs, check_vma=False
    )
```

profile of v0, /device:TPU:0, one launch (start us, length us, event | category | flops | bytes accessed | tf_op | source)
XLA Modules:
  0.0 191.5 jit_solution(7331570918606781942)
XLA Ops:
  1.6 1.4 fusion.66
  5.5 8.7 %shard_map.127 = bf16[96,2880]{1,0:T(8,128)(2,1)S(1)} custom-call(bf16[96,720]{1,0:T(8,128)(2,1)S(1)} %copy-done.1), custom_call_target="tpu_custom_call" | custom-call | bytes 4423680 | tf_op jit(solution)/shard_map/pallas_call | solution.py:109
  14.4 3.2 %fusion.41 = f32[96,512]{0,1:T(8,128)S(1)} fusion(bf16[2880,512]{1,0:T(8,128)(2,1)} %param.15, bf16[96,2880]{1,0:T(8,128)(2,1)S(1)} %shard_map.127, f32[2880]{0:T(1024)} %param.14, f32[96]{0:T(128)S(1)} %add_rsqrt_fusion), kind=kOutput, calls=%fused_computation.40 | convolution fusion | flops 284221440 | bytes 3710592 | tf_op jit(solution)/shard_map/dot_general | solution.py:392
  18.2 1.7 copy.107
  19.9 1.7 copy.108
  21.6 7.8 %fusion.72 = (f32[96,2,4]{2,1,0:T(2,128)}, f32[96,2,4,128]{3,2,1,0:T(4,128)}) fusion(bf16[96,2,128,128]{3,2,1,0:T(8,128)(2,1)} %param.19, bf16[96,2,4,32]{3,2,1,0:T(4,128)(2,1)} %bitcast.170, bf16[96,2,4,32]{3,2,1,0:T(4,128)(2,1)} %bitcast.168, pred[96,128]{1,0:T(8,128)(4,1)} %fusion.66), kind=kOutput, calls=%fused_computation.151 | convolution fusion | flops 13073664 | bytes 6798336 | tf_op jit(solution)/shard_map/skgh,skwh->skgw/dot_general | solution.py:408
  30.4 4.9 %copy.138 = bf16[2880,2,128]{0,2,1:T(8,128)(2,1)} copy(bf16[2880,2,128]{2,1,0:T(2,128)(2,1)} %param.16) | data formatting | bytes 2949120 | tf_op jit(solution)/shard_map/dot_general | solution.py:393
  35.3 2.0 %fusion.10 = f32[96,2,128]{2,0,1:T(8,128)S(1)} fusion(bf16[2880,2,128]{0,2,1:T(8,128)(2,1)} %copy.138, bf16[96,2880]{1,0:T(8,128)(2,1)S(1)} %shard_map.127, f32[2880]{0:T(1024)S(1)} %copy-done.9, f32[96]{0:T(128)S(1)} %add_rsqrt_fusion), kind=kOutput, calls=%fused_computation.11 | convolution fusion | flops 142663680 | bytes 2137728 | tf_op jit(solution)/shard_map/dot_general | solution.py:393
  40.9 1.4 fusion.68
  44.9 5.9 %fusion.25 = bf16[96,2,4,64]{3,2,1,0:T(4,128)(2,1)} fusion(bf16[96,2,128,128]{3,2,1,0:T(8,128)(2,1)} %param.19, f32[96,2,4,128]{3,2,1,0:T(4,128)S(1)} %copy-done.8, f32[96,2,64]{2,1,0:T(2,128)S(1)} %copy.122, f32[96,2,4]{2,1,0:T(2,128)S(1)} %copy.121, f32[96,2,4]{2,1,0:T(2,128)} %copy.119, f32[96,2,4]{2,1,0:T(2,128)S(1)} %copy.117), kind=kOutput, calls=%fused_computation.21 | convolution fusion | flops 13025280 | bytes 6841344 | tf_op jit(solution)/shard_map/skgw,skwh->skgh/dot_general | solution.py:427
  52.9 8.1 %shard_map.128 = f32[96,720]{1,0:T(8,128)S(1)} custom-call(bf16[4,96,720]{2,1,0:T(8,128)(2,1)S(1)} %fusion.18.x_ref), custom_call_target="tpu_custom_call" | custom-call | bytes 4423680 | tf_op jit(solution)/shard_map/pallas_call | solution.py:157
  62.4 5.5 %shard_map.129 = f32[96,9]{1,0:T(8,128)S(1)} custom-call(f32[1,96,9]{2,1,0:T(8,128)S(1)} %bitcast.164), custom_call_target="tpu_custom_call" | custom-call | bytes 55296 | tf_op jit(solution)/shard_map/pallas_call | solution.py:157
  68.6 31.3 %shard_map.130 = bf16[768,2880]{1,0:T(8,128)(2,1)S(1)} custom-call(bf16[96,720]{1,0:T(8,128)(2,1)S(1)} %multiply_convert_fusion.x_ref), custom_call_target="tpu_custom_call" | custom-call | bytes 17694720 | tf_op jit(solution)/shard_map/pallas_call | solution.py:331
  99.9 10.2 %fusion.73 = f32[768,1440]{1,0:T(8,128)S(1)} fusion(bf16[768,2880]{1,0:T(8,128)(2,1)S(1)} %shard_map.130, bf16[2880,1440]{0,1:T(8,128)(2,1)} %bitcast.174), kind=kOutput, calls=%fused_computation.152 | convolution fusion | flops 6370099200 | bytes 17141760 | tf_op jit(solution)/shard_map/dot_general | solution.py:466
  111.1 16.8 %shard_map.131 = bf16[384,2880]{1,0:T(8,128)(2,1)S(1)} custom-call(bf16[384,720]{1,0:T(8,128)(2,1)S(1)} %get-tuple-element.9.x_ref), custom_call_target="tpu_custom_call" | custom-call | bytes 17694720 | tf_op jit(solution)/shard_map/pallas_call | solution.py:109
  127.9 5.5 %fusion.12 = bf16[384,720]{0,1:T(8,128)(2,1)} fusion(bf16[384,2880]{1,0:T(8,128)(2,1)S(1)} %shard_map.131, bf16[1,2880,720]{1,2,0:T(8,128)(2,1)} %param.24), kind=kOutput, calls=%fused_computation.16 | convolution fusion | flops 1592801280 | bytes 6912000 | tf_op jit(solution)/shard_map/dot_general | solution.py:477
  133.4 2.1 %copy.130 = bf16[384,720]{1,0:T(8,128)(2,1)} copy(bf16[384,720]{0,1:T(8,128)(2,1)} %fusion.12) | data formatting | bytes 1105920 | tf_op jit(solution)/shard_map/convert_element_type | solution.py:478
  135.5 4.7 %all-to-all-start = ((bf16[8,1,48,720]{3,2,1,0:T(8,128)(2,1)}), bf16[8,1,48,720]{3,2,1,0:T(8,128)(2,1)}, u32[]{:S(2)}, u32[]{:S(2)}) async-start(bf16[8,1,48,720]{3,2,1,0:T(8,128)(2,1)} %bitcast.166), calls=%async_computation | async-start | bytes 1179648 | tf_op jit(solution)/shard_map/all_to_all | solution.py:479
  140.2 1.5 slice_multiply_fusion
  142.5 16.8 %shard_map.132 = bf16[384,2880]{1,0:T(8,128)(2,1)S(1)} custom-call(bf16[384,720]{1,0:T(8,128)(2,1)S(1)} %get-tuple-element.10.x_ref), custom_call_target="tpu_custom_call" | custom-call | bytes 17694720 | tf_op jit(solution)/shard_map/pallas_call | solution.py:109
  159.3 5.5 %fusion.15 = bf16[384,720]{0,1:T(8,128)(2,1)} fusion(bf16[384,2880]{1,0:T(8,128)(2,1)S(1)} %shard_map.132, bf16[1,2880,720]{1,2,0:T(8,128)(2,1)} %param.24), kind=kOutput, calls=%fused_computation.17 | convolution fusion | flops 1592801280 | bytes 6912000 | tf_op jit(solution)/shard_map/dot_general | solution.py:477
  164.8 2.2 %copy.131 = bf16[384,720]{1,0:T(8,128)(2,1)} copy(bf16[384,720]{0,1:T(8,128)(2,1)} %fusion.15) | data formatting | bytes 1105920 | tf_op jit(solution)/shard_map/convert_element_type | solution.py:478
  167.0 5.7 %all-to-all-start.1 = ((bf16[8,1,48,720]{3,2,1,0:T(8,128)(2,1)}), bf16[8,1,48,720]{3,2,1,0:T(8,128)(2,1)}, u32[]{:S(2)}, u32[]{:S(2)}) async-start(bf16[8,1,48,720]{3,2,1,0:T(8,128)(2,1)} %bitcast.165), calls=%async_computation.1 | async-start | bytes 1179648 | tf_op jit(solution)/shard_map/all_to_all | solution.py:479
  174.2 15.2 %all-to-all-done.1 = bf16[8,1,48,720]{3,2,1,0:T(8,128)(2,1)} async-done(((bf16[8,1,48,720]{3,2,1,0:T(8,128)(2,1)}), bf16[8,1,48,720]{3,2,1,0:T(8,128)(2,1)}, u32[]{:S(2)}, u32[]{:S(2)}) %all-to-all-start.1) | async-done | bytes 552992 | tf_op jit(solution)/shard_map/all_to_all | solution.py:479
  (71 shorter events, 21.4 us)
Async XLA Ops:
  0.0 51.9 %copy-start = (bf16[512,2880]{0,1:T(8,128)(2,1)S(1)}, bf16[512,2880]{0,1:T(8,128)(2,1)}, u32[]{:S(2)}) copy-start(bf16[512,2880]{0,1:T(8,128)(2,1)} %param.18) | copy-start | bytes 8847364
  0.9 39.1 %copy-start.12 = (f32[2,4]{1,0:T(2,128)}, f32[2,4]{1,0:T(2,128)S(1)}, u32[]{:S(2)}) copy-start(f32[2,4]{1,0:T(2,128)S(1)} %max.36) | copy-start | bytes 100
  4.6 0.9 copy-start.1
  29.4 5.9 %copy-start.9 = (f32[2880]{0:T(1024)S(1)}, f32[2880]{0:T(1024)}, u32[]{:S(2)}) copy-start(f32[2880]{0:T(1024)} %param.14) | copy-start | bytes 34564
  35.3 4.0 %copy-start.6 = (bf16[96,8,32]{2,1,0:T(8,128)(2,1)S(1)}, bf16[96,8,32]{2,1,0:T(8,128)(2,1)}, u32[]{:S(2)}) copy-start(bf16[96,8,32]{2,1,0:T(8,128)(2,1)} %copy.107) | copy-start | bytes 147460
  35.3 4.0 %copy-start.7 = (bf16[96,8,32]{2,1,0:T(8,128)(2,1)S(1)}, bf16[96,8,32]{2,1,0:T(8,128)(2,1)}, u32[]{:S(2)}) copy-start(bf16[96,8,32]{2,1,0:T(8,128)(2,1)} %copy.108) | copy-start | bytes 147460
  37.4 2.9 %copy-start.8 = (f32[96,2,4,128]{3,2,1,0:T(4,128)S(1)}, f32[96,2,4,128]{3,2,1,0:T(4,128)}, u32[]{:S(2)}) copy-start(f32[96,2,4,128]{3,2,1,0:T(4,128)} %get-tuple-element.38) | copy-start | bytes 1179652
  51.9 9.1 %copy-start.2 = (bf16[96,720]{1,0:T(8,128)(2,1)S(1)}, bf16[96,720]{1,0:T(8,128)(2,1)}, u32[]{:S(2)}) copy-start(bf16[96,720]{1,0:T(8,128)(2,1)} %x_ref.1) | copy-start | bytes 414724
  51.9 10.1 %copy-start.10 = (bf16[720,8]{0,1:T(8,128)(2,1)S(1)}, bf16[720,8]{0,1:T(8,128)(2,1)}, u32[]{:S(2)}) copy-start(bf16[720,8]{0,1:T(8,128)(2,1)} %param.22) | copy-start | bytes 34564
  61.2 38.8 %copy-start.4 = (f32[96,720]{1,0:T(8,128)}, f32[96,720]{1,0:T(8,128)S(1)}, u32[]{:S(2)}) copy-start(f32[96,720]{1,0:T(8,128)S(1)} %get-tuple-element.6) | copy-start | bytes 829444
  67.9 0.6 copy-start.3
  135.5 31.5 %all-to-all-start = ((bf16[8,1,48,720]{3,2,1,0:T(8,128)(2,1)}), bf16[8,1,48,720]{3,2,1,0:T(8,128)(2,1)}, u32[]{:S(2)}, u32[]{:S(2)}) async-start(bf16[8,1,48,720]{3,2,1,0:T(8,128)(2,1)} %bitcast.166), calls=%async_computation | async-start | bytes 1179648 | tf_op jit(solution)/shard_map/all_to_all | solution.py:479
  159.3 13.4 %copy-start.11 = (s32[96,4]{0,1:T(4,128)S(1)}, s32[96,4]{0,1:T(4,128)}, u32[]{:S(2)}) copy-start(s32[96,4]{0,1:T(4,128)} %param.25) | copy-start | bytes 4612
  164.8 8.1 %copy-start.5 = (f32[96,720]{1,0:T(8,128)S(1)}, f32[96,720]{1,0:T(8,128)}, u32[]{:S(2)}) copy-start(f32[96,720]{1,0:T(8,128)} %copy-done.4) | copy-start | bytes 829444
  167.0 22.4 %all-to-all-start.1 = ((bf16[8,1,48,720]{3,2,1,0:T(8,128)(2,1)}), bf16[8,1,48,720]{3,2,1,0:T(8,128)(2,1)}, u32[]{:S(2)}, u32[]{:S(2)}) async-start(bf16[8,1,48,720]{3,2,1,0:T(8,128)(2,1)} %bitcast.165), calls=%async_computation.1 | async-start | bytes 1179648 | tf_op jit(solution)/shard_map/all_to_all | solution.py:479
where the time goes:
time: 193 us; the launch traced here: 192 us
  Pallas kernels  87.2 us (45%)
  matrix products  41.4 us (21%)
  local copies, waits for them, and re-layouts  24 us (12%)
  waiting for transfers between devices  15.2 us (8%)
  other arithmetic  12.9 us (7%)
  starting transfers between devices  10.4 us (5%)
    pallas_call x3, Pallas kernels, feature_gather(): pl.pallas_call(functools.partial(feature_gather_kernel, tp, chunks), out_...  42.3 us
    pallas_call x1, Pallas kernels, full_gather(): pl.pallas_call(functools.partial(full_gather_kernel, dp, ny, tp), out_sha...  31.3 us
    all_to_all x2, waiting for transfers between devices, on_device(): lax.all_to_all(jnp.stack(outs, axis=1), 'dp', split_axis=0, concat_axis=0...  15.2 us
    pallas_call x2, Pallas kernels, share_sum(): pl.pallas_call(functools.partial(share_sum_kernel, tp, scatter), out_shap...  13.6 us
    dot_general x2, matrix products, on_device(): out = jnp.dot(act_all, w_down[e], preferred_element_type=jnp.float32)  10.9 us
    all_to_all x2, starting transfers between devices, on_device(): lax.all_to_all(jnp.stack(outs, axis=1), 'dp', split_axis=0, concat_axis=0...  10.4 us
    dot_general x1, matrix products, on_device(): jnp.dot(all_rows, gate_up_flat[e], preferred_element_type=jnp.float32)  10.2 us
    dot_general x1, matrix products, on_device(): jnp.einsum('skgh,skwh->skgw', grouped, window_cache[..., :head_size], pre...  7.85 us
  transfers between devices with their start and end apart: 2, of which 1 were waited for; matrix products, arithmetic and copies ran while one was open for 6% of the time, Pallas kernels for 9%

commit v1 on v0

--- a/solution.py
+++ b/solution.py
@@ -346,6 +346,307 @@
             collective_id=collective_id, has_side_effects=True, vmem_limit_bytes=48 * 2**20),
         cost_estimate=pl.CostEstimate(flops=0, bytes_accessed=rows * cols * dp * tp * 8, transcendentals=0),
     )(x)
+
+
+LANE = 128
+
+
+def pad_up(n, m):
+    return -(-n // m) * m
+
+
+def dot_t(a, b):
+    return lax.dot_general(a, b, (((1,), (1,)), ((), ())), preferred_element_type=jnp.float32)
+
+
+def moe_kernel(
+    dp, ny, tp, experts,
+    res_ref, gain_ref, router_ref, chosen_ref, gu_hbm, wd_hbm, out_ref,
+    rows_buf, gu_raw, gu_pad, wd_raw, wd_pad, act_buf, out_buf, back_buf,
+    load_sem, s_twin, s_x, s_y, s_z, r_rows, s_act, r_act, s_out, r_out,
+):
+    nz = dp // ny
+    dp_id = lax.axis_index("dp")
+    me = lax.axis_index("tp")
+    core, chip = lax.rem(me, CORES), me // CORES
+    z, y = dp_id // ny, lax.rem(dp_id, ny)
+    seq, wide = res_ref.shape
+    cols = out_ref.shape[1]
+    full = gu_hbm.shape[2]
+    twin_t = chip * CORES + 1 - core
+    across_t = (1 - chip) * CORES + core
+    corner_t = (1 - chip) * CORES + 1 - core
+    twin, across = (dp_id, twin_t), (dp_id, across_t)
+    y_peer = (z * ny + 1 - y, me)
+
+    gu_load = pltpu.make_async_copy(gu_hbm, gu_raw, load_sem.at[0])
+    wd_load = pltpu.make_async_copy(wd_hbm, wd_raw, load_sem.at[1])
+    gu_load.start()
+    wd_load.start()
+
+    barrier = pltpu.get_barrier_semaphore()
+    for d in range(1, dp):
+        pl.semaphore_signal(barrier, inc=1, device_id=(lax.rem(dp_id + d, dp), me), device_id_type=MESH)
+    for other in (twin, across):
+        pl.semaphore_signal(barrier, inc=1, device_id=other, device_id_type=MESH)
+
+    res = res_ref[...]
+    gained = res * gain_ref[...]
+    values = [jnp.sum(res * res, axis=1, keepdims=True)]
+    for e in range(experts):
+        values.append(jnp.sum(gained * router_ref[e:e + 1, :], axis=1, keepdims=True))
+    tail = cols - (wide - LANE)
+    lanes = lax.broadcasted_iota(jnp.int32, (seq, LANE), 1)
+    group = (LANE - tail) // 3
+    spread = jnp.zeros((seq, LANE), jnp.float32)
+    for j, v in enumerate(values):
+        for g in range(3):
+            spread = jnp.where(lanes == tail + g * group + j, v, spread)
+    high = spread.astype(jnp.bfloat16).astype(jnp.float32)
+    middle = (spread - high).astype(jnp.bfloat16).astype(jnp.float32)
+    low = spread - high - middle
+    last = jnp.where(lanes < tail, gained[:, wide - LANE:], jnp.where(
+        lanes < tail + group, high, jnp.where(lanes < tail + 2 * group, middle, low)))
+    rows_buf[dp_id, me, :, :wide - LANE] = gained[:, :wide - LANE].astype(jnp.bfloat16)
+    rows_buf[dp_id, me, :, wide - LANE:] = last.astype(jnp.bfloat16)
+
+    pl.semaphore_wait(barrier, dp + 1)
+
+    def piece(b, t, sem, target):
+        view = rows_buf.at[b, t]
+        return pltpu.make_async_remote_copy(
+            src_ref=view, dst_ref=view, send_sem=sem, recv_sem=r_rows.at[b, t],
+            device_id=target, device_id_type=MESH)
+
+    def to_twin(b, t):
+        return piece(b, t, s_twin.at[b, t], twin)
+
+    def to_y(b, t):
+        return piece(b, t, s_y.at[b, t // CORES], y_peer)
+
+    def to_z(t, d):
+        return piece(dp_id, t, s_z.at[t // CORES, d], (lax.rem(z + d, nz) * ny + y, me))
+
+    def arrived(b, t):
+        piece(b, t, r_rows.at[b, t], twin).wait_recv()
+
+    def plane(k):
+        near = jnp.minimum(z, nz - 1 - z)
+        step = (k + 1) // 2
+        swing = jnp.where(lax.rem(k, 2) == 1, z - step, z + step)
+        rest = jnp.where(z < nz - 1 - z, k, nz - 1 - k)
+        return jnp.where(k <= 2 * near, swing, rest)
+
+    piece(dp_id, me, s_x, across).start()
+    to_y(dp_id, me).start()
+    to_twin(dp_id, me).start()
+
+    def send_far(t):
+        def body(k, carry):
+            d = lax.rem(plane(k) - z + nz, nz)
+            to_z(t, d).start()
+            return carry
+        lax.fori_loop(1, nz, body, 0)
+
+    send_far(me)
+
+    gu_load.wait()
+    wd_load.wait()
+
+    def widen(raw, padded, lead):
+        block = 48
+        blocks = raw.shape[-2] // block
+
+        def body(i, carry):
+            at = pl.ds(pl.multiple_of(i * block, 16), block)
+            v = raw[lead + (at, slice(None))]
+            for t in range(tp):
+                part = v[:, t * cols:(t + 1) * cols]
+                padded[lead + (at, pl.ds(t * wide, wide))] = jnp.concatenate(
+                    [part, jnp.zeros((block, wide - cols), v.dtype)], axis=1)
+            return carry
+        lax.fori_loop(0, blocks, body, 0)
+        rest = padded.shape[-2] - raw.shape[-2]
+        padded[lead + (pl.ds(raw.shape[-2], rest), slice(None))] = jnp.zeros((rest, tp * wide), padded.dtype)
+
+    widen(gu_raw, gu_pad, (0,))
+    widen(gu_raw, gu_pad, (1,))
+
+    arrived(dp_id, across_t)
+    to_y(dp_id, across_t).start()
+    to_twin(dp_id, across_t).start()
+    send_far(across_t)
+    widen(wd_raw, wd_pad, ())
+
+    def far_arrival(k, t):
+        b = plane(k) * ny + y
+        arrived(b, t)
+        to_y(b, t).start()
+        to_twin(b, t).start()
+
+    def act_copy(t, p, sem, target):
+        view = act_buf.at[t, p]
+        return pltpu.make_async_remote_copy(
+            src_ref=view, dst_ref=view, send_sem=sem, recv_sem=r_act.at[t, p],
+            device_id=target, device_id_type=MESH)
+
+    def act_arrived(t, p):
+        act_copy(t, p, r_act.at[t, p], twin).wait_recv()
+
+    def out_copy(b):
+        return pltpu.make_async_remote_copy(
+            src_ref=out_buf.at[b], dst_ref=back_buf.at[dp_id], send_sem=s_out.at[b],
+            recv_sem=r_out.at[dp_id], device_id=(b, me), device_id_type=MESH)
+
+    def stats_tile(b):
+        total = rows_buf[b, 0, :, wide - LANE:].astype(jnp.float32)
+        for t in range(1, tp):
+            total = total + rows_buf[b, t, :, wide - LANE:].astype(jnp.float32)
+        total = jnp.where(lanes >= tail, total, 0.0)
+        return total
+
+    def row_scale(total):
+        hit = (lanes == tail) | (lanes == tail + group) | (lanes == tail + 2 * group)
+        squares = jnp.sum(jnp.where(hit, total, 0.0), axis=1, keepdims=True)
+        return lax.rsqrt(squares / full + norm_eps)
+
+    tile_n = 256
+    n_tiles = wide // tile_n
+
+    def up_project(p):
+        scale = jnp.concatenate([row_scale(stats_tile(p * ny + b)) for b in range(ny)], axis=0)
+
+        def body(n, carry):
+            at = pl.ds(pl.multiple_of(n * tile_n, tile_n), tile_n)
+            lhs = jnp.concatenate([
+                jnp.concatenate([rows_buf[p * ny + b, t] for t in range(tp)], axis=1)
+                for b in range(ny)], axis=0)
+            gate = dot_t(lhs, gu_pad[0, at, :]) * scale
+            up = dot_t(lhs, gu_pad[1, at, :]) * scale
+            act_buf[me, p, :, at] = (gate * jax.nn.sigmoid(glu_alpha * gate) * (up + 1.0)).astype(jnp.bfloat16)
+            return carry
+        lax.fori_loop(0, n_tiles, body, 0)
+
+    def down_project(p):
+        def body(n, carry):
+            at = pl.ds(pl.multiple_of(n * tile_n, tile_n), tile_n)
+            lhs = jnp.concatenate([act_buf[t, p] for t in range(tp)], axis=1)
+            out = dot_t(lhs, wd_pad[at, :]).astype(jnp.bfloat16)
+            for b in range(ny):
+                out_buf[p * ny + b, :, at] = out[b * seq:(b + 1) * seq]
+            return carry
+        lax.fori_loop(0, n_tiles, body, 0)
+
+    def stage(k, carry):
+        @pl.when(k < nz - 1)
+        def _():
+            far_arrival(k + 1, me)
+
+        @pl.when(k < nz)
+        def _():
+            p = plane(k)
+            for t in (me, across_t):
+                b = p * ny + 1 - y
+                arrived(b, t)
+                to_twin(b, t).start()
+            for b in range(ny):
+                for t in (twin_t, corner_t):
+                    arrived(p * ny + b, t)
+            up_project(p)
+            act_copy(me, p, s_act.at[0, p], across).start()
+            act_copy(me, p, s_act.at[1, p], twin).start()
+
+        @pl.when(k < nz - 1)
+        def _():
+            far_arrival(k + 1, across_t)
+
+        @pl.when(k > 0)
+        def _():
+            p = plane(k - 1)
+            act_arrived(across_t, p)
+            act_copy(across_t, p, s_act.at[2, p], twin).start()
+            act_arrived(twin_t, p)
+            act_arrived(corner_t, p)
+            down_project(p)
+            for b in range(ny):
+                @pl.when(p * ny + b != dp_id)
+                def _():
+                    out_copy(p * ny + b).start()
+
+                @pl.when(p * ny + b == dp_id)
+                def _():
+                    back_buf[dp_id] = out_buf[dp_id]
+        return carry
+
+    lax.fori_loop(0, nz + 1, stage, 0)
+
+    total = stats_tile(dp_id)
+    scale = row_scale(total)
+    shift = LANE - group
+    summed = total + pltpu.roll(total, shift, 1) + pltpu.roll(pltpu.roll(total, shift, 1), shift, 1)
+    chosen = chosen_ref[...]
+    raised = jnp.where(chosen > 0.0, jnp.exp(jnp.where(chosen > 0.0, summed * scale, 0.0)), 0.0)
+    weights = raised / jnp.sum(raised, axis=1, keepdims=True)
+
+    def wait_out(d, carry):
+        b = lax.rem(dp_id + d, dp)
+        pltpu.make_async_remote_copy(
+            src_ref=back_buf.at[b], dst_ref=back_buf.at[b], send_sem=r_out.at[b],
+            recv_sem=r_out.at[b], device_id=twin, device_id_type=MESH).wait_recv()
+        return carry
+
+    lax.fori_loop(1, dp, wait_out, 0)
+    answer = res
+    for e in range(dp):
+        answer = answer + weights[:, tail + 1 + e:tail + 2 + e] * back_buf[e].astype(jnp.float32)
+    out_ref[...] = answer[:, :cols]
+
+    piece(dp_id, me, s_x, across).wait_send()
+    for t in (me, across_t):
+        for d in range(1, nz):
+            to_z(t, d).wait_send()
+        for p in range(nz):
+            to_y(p * ny + y, t).wait_send()
+            for b in range(ny):
+                to_twin(p * ny + b, t).wait_send()
+    for p in range(nz):
+        act_copy(me, p, s_act.at[0, p], across).wait_send()
+        act_copy(me, p, s_act.at[1, p], twin).wait_send()
+        act_copy(across_t, p, s_act.at[2, p], twin).wait_send()
+    for d in range(1, dp):
+        out_copy(lax.rem(dp_id + d, dp)).wait_send()
+
+
+def moe(res, gain, router, chosen, gate_up, w_down, dp, ny, tp, collective_id):
+    seq, cols = res.shape
+    wide = pad_up(cols, 256)
+    full = gate_up.shape[2]
+    experts = router.shape[0]
+    nz = dp // ny
+    pad = ((0, 0), (0, wide - cols))
+    bf = jnp.bfloat16
+    dma = pltpu.SemaphoreType.DMA
+    return pl.pallas_call(
+        functools.partial(moe_kernel, dp, ny, tp, experts),
+        out_shape=jax.ShapeDtypeStruct((seq, cols), jnp.float32),
+        in_specs=[pl.BlockSpec(memory_space=pltpu.VMEM)] * 4 + [pl.BlockSpec(memory_space=pl.ANY)] * 2,
+        out_specs=pl.BlockSpec(memory_space=pltpu.VMEM),
+        scratch_shapes=[
+            pltpu.VMEM((dp, tp, seq, wide), bf),
+            pltpu.VMEM((2, cols, full), bf),
+            pltpu.VMEM((2, wide, tp * wide), bf),
+            pltpu.VMEM((cols, full), bf),
+            pltpu.VMEM((wide, tp * wide), bf),
+            pltpu.VMEM((tp, nz, ny * seq, wide), bf),
+            pltpu.VMEM((dp, seq, wide), bf),
+            pltpu.VMEM((dp, seq, wide), bf),
+            dma((2,)), dma((dp, tp)), dma, dma((dp, tp // CORES)), dma((tp // CORES, nz)), dma((dp, tp)),
+            dma((3, nz)), dma((tp, nz)), dma((dp,)), dma((dp,)),
+        ],
+        compiler_params=pltpu.CompilerParams(
+            collective_id=collective_id, has_side_effects=True, vmem_limit_bytes=56 * 2**20),
+        cost_estimate=pl.CostEstimate(flops=6 * dp * seq * full * cols, bytes_accessed=6 * full * cols, transcendentals=0),
+    )(jnp.pad(res, pad), jnp.pad(gain[None, :], pad), jnp.pad(router, pad), chosen, gate_up, w_down)
 
 
 def activate(mixed_in, ff_local):
@@ -440,6 +741,16 @@
     local_experts = gate_up.shape[0]
     ff_local = gate_up.shape[3]
     capacity = min(seq_count, max(2, 8 * seq_count * top_count // (3 * experts)))
+    expert_iota = jnp.arange(experts, dtype=jnp.int32)
+    nz_ny = 2 ** (int(math.log2(dp_count)) // 2)
+    if capacity >= seq_count and local_experts == 1 and nz_ny == 2 and tp_count == 2 * CORES:
+        wide = pad_up(col_count, 256)
+        first = col_count - (wide - LANE) + 1
+        lane_iota = jnp.arange(LANE, dtype=jnp.int32) - first
+        chosen_lanes = jnp.any(expert_ids[:, :, None] == lane_iota[None, None, :], axis=1).astype(jnp.float32)
+        return moe(
+            residual, moe_slice, router.T.astype(jnp.float32), chosen_lanes,
+            jnp.transpose(gate_up[0], (1, 2, 0)), w_down[0].T, dp_count, nz_ny, tp_count, 1)
     moe_sq = jnp.sum(residual * residual, axis=1)
     router_wide = router.astype(jnp.float32)
     gained = residual * moe_slice[None, :]
@@ -450,7 +761,6 @@
     moe_scale = lax.rsqrt(stats[:, :1] / full_width + norm_eps)
     logits = stats[:, 1:] * moe_scale
     hidden_rows = (gained * moe_scale).astype(jnp.bfloat16)
-    expert_iota = jnp.arange(experts, dtype=jnp.int32)
     chosen = expert_ids[:, :, None] == expert_iota[None, None, :]
     picked = jnp.sum(jnp.where(chosen, logits[:, None, :], 0.0), axis=-1)
     raised_logits = jnp.exp(picked)

time: 193 us -> 148 us (0.77)
  matrix products: 41.4 us -> 19.1 us
  Pallas kernels: 87.2 us -> 105 us
  waiting for transfers between devices: 15.2 us -> 0 us
  starting transfers between devices: 10.4 us -> 0 us
  local copies, waits for them, and re-layouts: 24 us -> 14.9 us
  other arithmetic: 12.9 us -> 7.31 us
    pallas_call x1, Pallas kernels: 31.3 us -> 87.7 us  [moe(): pl.pallas_call(functools.partial(moe_kernel, dp, ny, tp, experts), out_sh...]
    pallas_call x3 -> x1, Pallas kernels: 42.3 us -> 8.7 us  [feature_gather(): pl.pallas_call(functools.partial(feature_gather_kernel, tp, chunks), out_...]
    dot_general x4 -> x0, matrix products: 21.4 us -> none  [the longest x2 10.9 us: on_device(): out = jnp.dot(act_all, w_down[e], preferred_element_type=jnp.float32)]
    all_to_all x2 -> x0, waiting for transfers between devices: 15.2 us -> none  [on_device(): lax.all_to_all(jnp.stack(outs, axis=1), 'dp', split_axis=0, concat_axis=0...]
    all_to_all x2 -> x0, starting transfers between devices: 10.4 us -> none  [on_device(): lax.all_to_all(jnp.stack(outs, axis=1), 'dp', split_axis=0, concat_axis=0...]
    pallas_call x2 -> x1, Pallas kernels: 13.6 us -> 8.08 us  [share_sum(): pl.pallas_call(functools.partial(share_sum_kernel, tp, scatter), out_shap...]
    convert_element_type x2 -> x0, local copies, waits for them, and re-layouts: 4.29 us -> none  [on_device(): outs.append(out.astype(jnp.bfloat16).reshape(dp_count, half, col_count))]
    another operation x2, local copies, waits for them, and re-layouts: 3.32 us -> 0.33 us
  transfers between devices with their start and end apart: 2 -> 0, of which waited for: 1 -> 0; matrix products, arithmetic and copies ran while one was open for 6% -> 0% of each run, Pallas kernels for 9% -> 0%
where the time goes in v1:
time: 148 us; the launch traced here: 146 us
  Pallas kernels  105 us (71%)
  matrix products  19.1 us (13%)
  local copies, waits for them, and re-layouts  14.9 us (10%)
  other arithmetic  7.31 us (5%)
    pallas_call x1, Pallas kernels, moe(): pl.pallas_call(functools.partial(moe_kernel, dp, ny, tp, experts), out_sh...  87.7 us
    pallas_call x1, Pallas kernels, feature_gather(): pl.pallas_call(functools.partial(feature_gather_kernel, tp, chunks), out_...  8.7 us
    pallas_call x1, Pallas kernels, share_sum(): pl.pallas_call(functools.partial(share_sum_kernel, tp, scatter), out_shap...  8.08 us
    dot_general x1, matrix products, on_device(): jnp.einsum('skgh,skwh->skgw', grouped, window_cache[..., :head_size], pre...  7.02 us
    dot_general x1, matrix products, on_device(): jnp.einsum('skgw,skwh->skgh', prob_bf, window_cache[..., head_size:], pre...  5.33 us
    dot_general x1, local copies, waits for them, and re-layouts, on_device(): jnp.dot(piece_rows, kv_flat, preferred_element_type=jnp.float32)  4.87 us
    dot_general x1, matrix products, on_device(): queries = jnp.dot(piece_rows, w_query, preferred_element_type=jnp.float32)  3.15 us

profile of v1, /device:TPU:0, one launch (start us, length us, event | category | flops | bytes accessed | tf_op | source)
XLA Modules:
  0.0 146.1 jit_solution(10949604756773092011)
XLA Ops:
  0.0 1.1 copy-done.1
  1.1 8.7 %shard_map.127 = bf16[96,2880]{1,0:T(8,128)(2,1)S(1)} custom-call(bf16[96,720]{1,0:T(8,128)(2,1)S(1)} %copy-done.1), custom_call_target="tpu_custom_call" | custom-call | bytes 4423680 | tf_op jit(solution)/shard_map/pallas_call | solution.py:109
  10.0 4.9 %copy.86 = bf16[2880,2,128]{0,2,1:T(8,128)(2,1)} copy(bf16[2880,2,128]{2,1,0:T(2,128)(2,1)} %param.16) | data formatting | bytes 2949120 | tf_op jit(solution)/shard_map/dot_general | solution.py:694
  14.9 2.6 %fusion.4 = f32[96,2,128]{2,0,1:T(8,128)} fusion(bf16[2880,2,128]{0,2,1:T(8,128)(2,1)} %copy.86, bf16[96,2880]{1,0:T(8,128)(2,1)S(1)} %shard_map.127, f32[2880]{0:T(1024)S(1)} %copy-done.4, f32[96]{0:T(128)S(1)} %add_rsqrt_fusion), kind=kOutput, calls=%fused_computation.4 | convolution fusion | flops 142663680 | bytes 2137728 | tf_op jit(solution)/shard_map/dot_general | solution.py:694
  18.2 0.7 copy.68
  18.9 0.7 copy.69
  19.6 1.1 fusion.31
  20.7 1.0 fusion.33
  21.8 0.7 slice_bitcast_fusion.1
  22.5 0.7 copy.70
  23.2 3.2 %fusion.27 = f32[96,512]{0,1:T(8,128)S(1)} fusion(bf16[2880,512]{1,0:T(8,128)(2,1)} %param.15, bf16[96,2880]{1,0:T(8,128)(2,1)S(1)} %shard_map.127, f32[2880]{0:T(1024)} %param.14, f32[96]{0:T(128)S(1)} %add_rsqrt_fusion), kind=kOutput, calls=%fused_computation.27 | convolution fusion | flops 284221440 | bytes 3710592 | tf_op jit(solution)/shard_map/dot_general | solution.py:693
  26.7 1.4 multiply_reduce_fusion
  28.2 0.7 fusion.37
  29.0 7.0 %fusion.42 = (f32[96,2,4]{2,1,0:T(2,128)S(1)}, f32[96,2,4,128]{3,2,1,0:T(4,128)}) fusion(bf16[96,2,128,128]{3,2,1,0:T(8,128)(2,1)} %param.19, bf16[96,2,4,32]{3,2,1,0:T(4,128)(2,1)S(1)} %bitcast.44, bf16[96,2,4,32]{3,2,1,0:T(4,128)(2,1)S(1)} %bitcast.42, pred[96,128]{1,0:T(8,128)(4,1)S(1)} %fusion.37), kind=kOutput, calls=%fused_computation.66 | convolution fusion | flops 13073664 | bytes 6798336 | tf_op jit(solution)/shard_map/skgh,skwh->skgw/dot_general | solution.py:709
  36.4 1.6 %fusion.23 = f32[96,2,4]{2,1,0:T(2,128)S(1)} fusion(f32[96,2,4,128]{3,2,1,0:T(4,128)} %get-tuple-element.18, f32[96,2,4]{2,1,0:T(2,128)S(1)} %copy.73), kind=kLoop, calls=%fused_computation.21 | loop fusion | flops 195840 | bytes 399360 | tf_op jit(solution)/shard_map/reduce_sum | solution.py:724
  38.5 5.3 %fusion.13 = bf16[96,2,4,64]{3,2,1,0:T(4,128)(2,1)S(1)} fusion(bf16[96,2,128,128]{3,2,1,0:T(8,128)(2,1)} %param.19, f32[96,2,4,128]{3,2,1,0:T(4,128)} %get-tuple-element.18, f32[96,2,64]{2,1,0:T(2,128)S(1)} %copy.78, f32[96,2,4]{2,1,0:T(2,128)S(1)} %copy.77, f32[96,2,4]{2,1,0:T(2,128)S(1)} %copy.75, f32[96,2,4]{2,1,0:T(2,128)S(1)} %copy.73), kind=kOutput, calls=%fused_computation.12 | convolution fusion | flops 13025280 | bytes 6841344 | tf_op jit(solution)/shard_map/skgw,skwh->skgh/dot_general | solution.py:728
  44.1 1.0 fusion.6.x_ref
  45.1 8.1 %shard_map.128 = f32[96,720]{1,0:T(8,128)S(1)} custom-call(bf16[4,96,720]{2,1,0:T(8,128)(2,1)S(1)} %fusion.6.x_ref), custom_call_target="tpu_custom_call" | custom-call | bytes 4423680 | tf_op jit(solution)/shard_map/pallas_call | solution.py:157
  53.2 0.7 pad.14.res_ref
  54.0 0.8 dynamic_slice.3
  55.5 0.6 convert_element_type.88.chosen_ref
  56.1 0.6 pad_convert_fusion.router_ref
  56.7 87.7 %shard_map.129 = f32[96,720]{1,0:T(8,128)} custom-call(f32[96,768]{1,0:T(8,128)} %pad.14.res_ref, f32[1,768]{1,0:T(1,128)} %pad.15.gain_ref, f32[8,768]{1,0:T(8,128)} %pad_convert_fusion.router_ref, f32[96,128]{1,0:T(8,128)} %convert_element_type.88.chosen_ref, bf16[2,720,2880]{2,1,0:T(8,128)(2,1)} %bitcast.47, bf16[720,2880]{1,0:T(8,128)(2,1)} %bitcast.48), custom_call_target="tpu_custom_call" | custom-call | flops 9555148800 | bytes 12441600 | tf_op jit(solution)/shard_map/pallas_call | solution.py:629
  144.4 1.7 %copy.91 = f32[96,720]{1,0:T(8,128)} copy(f32[96,720]{1,0:T(8,128)} %shard_map.129) | data formatting | bytes 552960
  (42 shorter events, 3.3 us)
Async XLA Ops:
  0.0 44.0 %copy-start = (bf16[512,2880]{0,1:T(8,128)(2,1)S(1)}, bf16[512,2880]{0,1:T(8,128)(2,1)}, u32[]{:S(2)}) copy-start(bf16[512,2880]{0,1:T(8,128)(2,1)} %param.18) | copy-start | bytes 8847364
  0.0 1.1 copy-start.1
  1.1 13.8 %copy-start.4 = (f32[2880]{0:T(1024)S(1)}, f32[2880]{0:T(1024)}, u32[]{:S(2)}) copy-start(f32[2880]{0:T(1024)} %param.14) | copy-start | bytes 34564
  9.8 7.7 %copy-start.7 = (s32[96]{0:T(128)S(1)}, s32[96]{0:T(128)}, u32[]{:S(2)}) copy-start(s32[96]{0:T(128)} %param.20) | copy-start | bytes 1156
  28.9 7.1 %copy-start.8 = (f32[8]{0:T(128)S(1)}, f32[8]{0:T(128)}, u32[]{:S(2)}) copy-start(f32[8]{0:T(128)} %param.17) | copy-start | bytes 100
  29.0 9.5 %copy-start.3 = (f32[96,2,64]{2,0,1:T(8,128)S(1)}, f32[96,2,64]{2,0,1:T(8,128)}, u32[]{:S(2)}) copy-start(f32[96,2,64]{2,0,1:T(8,128)} %get-tuple-element.12) | copy-start | bytes 147460
  43.8 9.3 %copy-start.2 = (bf16[96,720]{1,0:T(8,128)(2,1)S(1)}, bf16[96,720]{1,0:T(8,128)(2,1)}, u32[]{:S(2)}) copy-start(bf16[96,720]{1,0:T(8,128)(2,1)} %x_ref.1) | copy-start | bytes 414724
  44.0 11.3 %copy-start.6 = (s32[96,4]{0,1:T(4,128)S(1)}, s32[96,4]{0,1:T(4,128)}, u32[]{:S(2)}) copy-start(s32[96,4]{0,1:T(4,128)} %param.25) | copy-start | bytes 4612
  44.1 12.0 %copy-start.5 = (bf16[720,8]{0,1:T(8,128)(2,1)S(1)}, bf16[720,8]{0,1:T(8,128)(2,1)}, u32[]{:S(2)}) copy-start(bf16[720,8]{0,1:T(8,128)(2,1)} %param.22) | copy-start | bytes 34564

commit v2 on v1

--- a/solution.py
+++ b/solution.py
@@ -3,6 +3,7 @@
 
 import jax
 import jax.numpy as jnp
+import numpy as np
 from jax import lax
 from jax.experimental import pallas as pl
 from jax.experimental.pallas import tpu as pltpu
@@ -361,7 +362,7 @@
 
 def moe_kernel(
     dp, ny, tp, experts,
-    res_ref, gain_ref, router_ref, chosen_ref, gu_hbm, wd_hbm, out_ref,
+    res_ref, gain_ref, router_ref, ids_ref, gu_hbm, wd_hbm, out_ref,
     rows_buf, gu_raw, gu_pad, wd_raw, wd_pad, act_buf, out_buf, back_buf,
     load_sem, s_twin, s_x, s_y, s_z, r_rows, s_act, r_act, s_out, r_out,
 ):
@@ -391,10 +392,15 @@
         pl.semaphore_signal(barrier, inc=1, device_id=other, device_id_type=MESH)
 
     res = res_ref[...]
-    gained = res * gain_ref[...]
+    gain = gain_ref[:, :cols]
+    for t in range(1, tp):
+        gain = jnp.where(me == t, gain_ref[:, t * cols:(t + 1) * cols], gain)
+    gained = res * jnp.concatenate([gain, jnp.zeros((1, wide - cols), jnp.float32)], axis=1)
     values = [jnp.sum(res * res, axis=1, keepdims=True)]
+    router = jnp.concatenate(
+        [router_ref[...].astype(jnp.float32), jnp.zeros((experts, wide - cols), jnp.float32)], axis=1)
     for e in range(experts):
-        values.append(jnp.sum(gained * router_ref[e:e + 1, :], axis=1, keepdims=True))
+        values.append(jnp.sum(gained * router[e:e + 1, :], axis=1, keepdims=True))
     tail = cols - (wide - LANE)
     lanes = lax.broadcasted_iota(jnp.int32, (seq, LANE), 1)
     group = (LANE - tail) // 3
@@ -584,8 +590,13 @@
     scale = row_scale(total)
     shift = LANE - group
     summed = total + pltpu.roll(total, shift, 1) + pltpu.roll(pltpu.roll(total, shift, 1), shift, 1)
-    chosen = chosen_ref[...]
-    raised = jnp.where(chosen > 0.0, jnp.exp(jnp.where(chosen > 0.0, summed * scale, 0.0)), 0.0)
+    square = lax.broadcasted_iota(jnp.int32, (seq, seq), 0) == lax.broadcasted_iota(jnp.int32, (seq, seq), 1)
+    chosen = lanes < 0
+    for k in range(ids_ref.shape[0]):
+        named = ids_ref[k:k + 1, :].astype(jnp.float32)
+        named = jnp.sum(jnp.where(square, named, 0.0), axis=1, keepdims=True).astype(jnp.int32)
+        chosen = chosen | (lanes == named + tail + 1)
+    raised = jnp.where(chosen, jnp.exp(jnp.where(chosen, summed * scale, 0.0)), 0.0)
     weights = raised / jnp.sum(raised, axis=1, keepdims=True)
 
     def wait_out(d, carry):
@@ -617,13 +628,12 @@
         out_copy(lax.rem(dp_id + d, dp)).wait_send()
 
 
-def moe(res, gain, router, chosen, gate_up, w_down, dp, ny, tp, collective_id):
-    seq, cols = res.shape
-    wide = pad_up(cols, 256)
+def moe(res, gain, router, ids, gate_up, w_down, dp, ny, tp, collective_id):
+    seq, wide = res.shape
+    cols = gain.shape[0] // tp
     full = gate_up.shape[2]
     experts = router.shape[0]
     nz = dp // ny
-    pad = ((0, 0), (0, wide - cols))
     bf = jnp.bfloat16
     dma = pltpu.SemaphoreType.DMA
     return pl.pallas_call(
@@ -646,7 +656,235 @@
         compiler_params=pltpu.CompilerParams(
             collective_id=collective_id, has_side_effects=True, vmem_limit_bytes=56 * 2**20),
         cost_estimate=pl.CostEstimate(flops=6 * dp * seq * full * cols, bytes_accessed=6 * full * cols, transcendentals=0),
-    )(jnp.pad(res, pad), jnp.pad(gain[None, :], pad), jnp.pad(router, pad), chosen, gate_up, w_down)
+    )(res, gain[None, :], router, ids, gate_up, w_down)
+
+
+def attend_kernel(
+    tp, kv_heads, group_size, head_size,
+    tok_ref, gain_ref, inverse_ref, pos_ref, sink_ref, wq_hbm, wkv_hbm, wo_hbm, cache_hbm, out_ref,
+    tok_buf, wq_buf, wkv_raw, wkv_wide, wkv_buf, wo_buf, cache_buf, q_rows, new_rows, pos_rows, att_rows,
+    part_buf, got_buf, load_sem, send_sem, recv_tok, recv_part,
+):
+    dp_id = lax.axis_index("dp")
+    me = lax.axis_index("tp")
+    core, chip = lax.rem(me, CORES), me // CORES
+    seq, cols = tok_ref.shape
+    wide = out_ref.shape[1]
+    window = cache_hbm.shape[2]
+    heads = kv_heads * group_size
+    twin_t = chip * CORES + 1 - core
+    across_t = (1 - chip) * CORES + core
+    corner_t = (1 - chip) * CORES + 1 - core
+    twin, across = (dp_id, twin_t), (dp_id, across_t)
+
+    loads = [
+        pltpu.make_async_copy(src, dst, load_sem.at[i]) for i, (src, dst) in enumerate(
+            [(wkv_hbm, wkv_raw), (wq_hbm, wq_buf), (cache_hbm, cache_buf), (wo_hbm, wo_buf)])
+    ]
+    for load in loads:
+        load.start()
+    own = pltpu.make_async_copy(tok_ref, tok_buf.at[me], load_sem.at[4])
+    own.start()
+    greet([twin, across])
+
+    def token_copy(src, t, i, target):
+        return pltpu.make_async_remote_copy(
+            src_ref=src, dst_ref=tok_buf.at[t], send_sem=send_sem.at[i], recv_sem=recv_tok.at[t],
+            device_id=target, device_id_type=MESH)
+
+    def token_arrived(t):
+        token_copy(tok_buf.at[t], t, 0, twin).wait_recv()
+
+    sent = [token_copy(tok_ref, me, 0, across), token_copy(tok_ref, me, 1, twin)]
+    for copy in sent:
+        copy.start()
+
+    lanes = lax.broadcasted_iota(jnp.int32, (seq, LANE), 1)
+
+    def column(row):
+        n = row.shape[1]
+        square = lax.broadcasted_iota(jnp.int32, (n, n), 0) == lax.broadcasted_iota(jnp.int32, (n, n), 1)
+        return jnp.sum(jnp.where(square, row, 0.0), axis=1, keepdims=True)
+
+    position = jnp.broadcast_to(column(pos_ref[...].astype(jnp.float32)), (seq, LANE))
+    angles = position * inverse_ref[...]
+    cosine = jnp.cos(angles)
+    front = lax.rem(lanes, head_size) < head_size // 2
+    sine = jnp.where(front, -jnp.sin(angles), jnp.sin(angles))
+    for h in range(heads):
+        pos_rows[pl.ds(h, seq, stride=heads), :] = position
+    sink = jnp.broadcast_to(column(sink_ref[...]), (heads, LANE))
+    sink = jnp.concatenate([sink] * 8, axis=0)
+
+    loads[0].wait()
+    kv_rows = wkv_raw.shape[0]
+    step = kv_rows // 30
+
+    def split(i, carry):
+        at = pl.multiple_of(i * step, 16)
+        wkv_wide[...] = wkv_raw[pl.ds(at, step), :].astype(jnp.float32)
+        half = pl.ds(pl.multiple_of(i * (step // kv_heads), 16), step // kv_heads)
+        for h in range(kv_heads):
+            wkv_buf[half, h * LANE:(h + 1) * LANE] = wkv_wide[
+                pl.ds(h, step // kv_heads, stride=kv_heads), :].astype(jnp.bfloat16)
+        return carry
+    lax.fori_loop(0, 30, split, 0)
+
+    token_arrived(across_t)
+    forward = token_copy(tok_buf.at[across_t], across_t, 2, twin)
+    forward.start()
+    sent.append(forward)
+    own.wait()
+    token_arrived(twin_t)
+    token_arrived(corner_t)
+    loads[1].wait()
+
+    pieces = [tok_buf[t].astype(jnp.float32) for t in range(tp)]
+    squares = jnp.sum(pieces[0] * pieces[0], axis=1, keepdims=True)
+    for v in pieces[1:]:
+        squares = squares + jnp.sum(v * v, axis=1, keepdims=True)
+    scale = lax.rsqrt(squares / (tp * cols) + norm_eps)
+    queries, fresh = 0.0, 0.0
+    for t in range(tp):
+        at = slice(t * cols, (t + 1) * cols)
+        normed = (pieces[t] * scale * gain_ref[:, at]).astype(jnp.bfloat16)
+        queries = queries + jnp.dot(normed, wq_buf[at, :], preferred_element_type=jnp.float32)
+        fresh = fresh + jnp.dot(normed, wkv_buf[at, :], preferred_element_type=jnp.float32)
+
+    def turned(v):
+        swapped = jnp.where(
+            front, pltpu.roll(v, LANE - head_size // 2, 1), pltpu.roll(v, head_size // 2, 1))
+        return v * cosine + swapped * sine
+
+    def rounded(v):
+        return v.astype(jnp.bfloat16).astype(jnp.float32)
+
+    low = lanes < head_size
+    for h in range(heads):
+        if h % 2 == 0:
+            pair = rounded(turned(queries[:, h // 2 * LANE:(h // 2 + 1) * LANE]))
+        if h % group_size == 0:
+            k = h // group_size
+            entry = fresh[:, k * LANE:(k + 1) * LANE]
+            entry = rounded(jnp.where(low, turned(entry), entry))
+        own_q = pair if h % 2 == 0 else pltpu.roll(pair, head_size, 1)
+        q_rows[pl.ds(h, seq, stride=heads), :] = jnp.where(low, own_q, 0.0)
+        new_rows[pl.ds(h, seq, stride=heads), :] = entry
+
+    loads[2].wait()
+    batch = 8
+    rows = batch * heads
+    slot = lax.broadcasted_iota(jnp.int32, (rows, LANE), 1)
+    upper = lax.broadcasted_iota(jnp.int32, (heads, LANE), 0) < group_size
+    score_scale = head_size ** (-0.5)
+
+    def attend(i, carry):
+        at = pl.ds(pl.multiple_of(i * rows, rows), rows)
+        q = q_rows[at, :]
+        entry = new_rows[at, :]
+        pos = pos_rows[at, :].astype(jnp.int32)
+        raw = []
+        for s in range(batch):
+            qs = q[s * heads:(s + 1) * heads]
+            lhs = jnp.concatenate(
+                [jnp.where(upper, qs, 0.0), jnp.where(upper, 0.0, qs)], axis=1).astype(jnp.bfloat16)
+            rhs = jnp.concatenate([cache_buf[i * batch + s, k] for k in range(kv_heads)], axis=1)
+            raw.append(dot_t(lhs, rhs))
+        scores = jnp.concatenate(raw, axis=0) * score_scale
+        fresh_score = jnp.sum(q * entry, axis=1, keepdims=True) * score_scale
+        current = slot == lax.rem(pos, window)
+        scores = jnp.where(current, fresh_score, jnp.where(slot <= pos, scores, -jnp.inf))
+        peak = jnp.maximum(jnp.max(scores, axis=1, keepdims=True), sink)
+        raised = jnp.exp(scores - peak)
+        denominator = jnp.sum(raised, axis=1, keepdims=True) + jnp.exp(sink - peak)
+        probs = rounded(raised / denominator)
+        fresh_prob = jnp.sum(jnp.where(current, probs, 0.0), axis=1, keepdims=True)
+        probs = jnp.where(current, 0.0, probs)
+        mixed = []
+        for s in range(batch):
+            lhs = probs[s * heads:(s + 1) * heads].astype(jnp.bfloat16)
+            rhs = jnp.concatenate([cache_buf[i * batch + s, k] for k in range(kv_heads)], axis=1)
+            both = jnp.dot(lhs, rhs, preferred_element_type=jnp.float32)
+            mixed.append(jnp.where(upper, both[:, :LANE], both[:, LANE:]))
+        att_rows[at, :] = jnp.concatenate(mixed, axis=0) + fresh_prob * entry
+        return carry
+
+    lax.fori_loop(0, seq // batch, attend, 0)
+
+    tiles = []
+    for j in range(heads // 2):
+        even = att_rows[pl.ds(2 * j, seq, stride=heads), :]
+        odd = att_rows[pl.ds(2 * j + 1, seq, stride=heads), :]
+        tiles.append(jnp.where(low, pltpu.roll(even, head_size, 1), odd).astype(jnp.bfloat16))
+    attended = jnp.concatenate(tiles, axis=1)
+    loads[3].wait()
+
+    def share(t):
+        return dot_t(attended, wo_buf[pl.ds(pl.multiple_of(t * cols, 16), cols), :])
+
+    def part_copy(i, target):
+        return pltpu.make_async_remote_copy(
+            src_ref=part_buf.at[i], dst_ref=got_buf.at[i], send_sem=send_sem.at[3 + i],
+            recv_sem=recv_part.at[i], device_id=target, device_id_type=MESH)
+
+    parts = [part_copy(0, twin), part_copy(1, across), part_copy(2, twin)]
+    part_buf[0] = share(corner_t).astype(jnp.bfloat16)
+    parts[0].start()
+    far = share(across_t)
+    parts[0].wait_recv()
+    part_buf[1] = (far + got_buf[0].astype(jnp.float32)).astype(jnp.bfloat16)
+    parts[1].start()
+    part_buf[2] = share(twin_t).astype(jnp.bfloat16)
+    parts[2].start()
+    total = tok_ref[...].astype(jnp.float32) + share(me)
+    parts[2].wait_recv()
+    total = total + got_buf[2].astype(jnp.float32)
+    parts[1].wait_recv()
+    total = total + got_buf[1].astype(jnp.float32)
+    out_ref[...] = jnp.concatenate([total, jnp.zeros((seq, wide - cols), jnp.float32)], axis=1)
+    for copy in sent + parts:
+        copy.wait_send()
+
+
+def attend_block(tokens, gain, positions, sinks, w_query, w_keyvalue, w_out, cache, tp, collective_id):
+    seq, cols = tokens.shape
+    wide = pad_up(cols, 256)
+    full = tp * cols
+    kv_heads, window, entry = cache.shape[1:]
+    head_size = entry // 2
+    heads = w_query.shape[1] // head_size
+    exponent = np.arange(LANE) % (head_size // 2) * (2.0 / head_size)
+    inverse = jnp.asarray(rope_base ** -exponent, jnp.float32)[None, :]
+    bf, f32 = jnp.bfloat16, jnp.float32
+    dma = pltpu.SemaphoreType.DMA
+    return pl.pallas_call(
+        functools.partial(attend_kernel, tp, kv_heads, heads // kv_heads, head_size),
+        out_shape=jax.ShapeDtypeStruct((seq, wide), f32),
+        in_specs=[pl.BlockSpec(memory_space=pltpu.VMEM)] * 5 + [pl.BlockSpec(memory_space=pl.ANY)] * 4,
+        out_specs=pl.BlockSpec(memory_space=pltpu.VMEM),
+        scratch_shapes=[
+            pltpu.VMEM((tp, seq, cols), bf),
+            pltpu.VMEM(w_query.shape, bf),
+            pltpu.VMEM((full * kv_heads, LANE), bf),
+            pltpu.VMEM((full * kv_heads // 30, LANE), f32),
+            pltpu.VMEM((full, kv_heads * LANE), bf),
+            pltpu.VMEM((full, heads * head_size), bf),
+            pltpu.VMEM(cache.shape, bf),
+            pltpu.VMEM((seq * heads, LANE), f32),
+            pltpu.VMEM((seq * heads, LANE), f32),
+            pltpu.VMEM((seq * heads, LANE), f32),
+            pltpu.VMEM((seq * heads, LANE), f32),
+            pltpu.VMEM((3, seq, cols), bf),
+            pltpu.VMEM((3, seq, cols), bf),
+            dma((5,)), dma((6,)), dma((tp,)), dma((3,)),
+        ],
+        compiler_params=pltpu.CompilerParams(
+            collective_id=collective_id, has_side_effects=True, vmem_limit_bytes=63 * 2**20),
+        cost_estimate=pl.CostEstimate(
+            flops=2 * seq * full * heads * head_size * 3, bytes_accessed=8 * full * heads * head_size,
+            transcendentals=0),
+    )(tokens, gain[None, :], inverse, positions[None, :], sinks[None, :],
+      w_query, w_keyvalue.reshape(full * kv_heads, LANE), w_out.T, cache)
 
 
 def activate(mixed_in, ff_local):
@@ -682,6 +920,15 @@
     q_local = w_query.shape[1] // head_size
     group_size = q_local // kv_local
     window = window_cache.shape[2]
+    experts = router.shape[1]
+    ny = 2 ** (int(math.log2(dp_count)) // 2)
+    if (tp_count, ny, gate_up.shape[0], kv_local, group_size, window, 2 * head_size) == (
+            2 * CORES, 2, 1, 2, 4, LANE, LANE):
+        residual = attend_block(
+            tokens, attn_gain, positions, attn_sinks, w_query, w_keyvalue, w_out, window_cache, tp_count, 0)
+        return moe(
+            residual, moe_gain, router.T, expert_ids.T, jnp.transpose(gate_up[0], (1, 2, 0)), w_down[0].T,
+            dp_count, ny, tp_count, 1)
     moe_slice = lax.dynamic_slice_in_dim(moe_gain, col_start, col_count)
     tok_wide = tokens.astype(jnp.float32)
     kv_flat = w_keyvalue.reshape(full_width, kv_local * 2 * head_size)
@@ -736,21 +983,10 @@
         preferred_element_type=jnp.float32,
     ).astype(jnp.bfloat16)
     residual = tok_wide + share_sum(partial_out, tp_count, True, 2)
-    experts = router.shape[1]
     top_count = expert_ids.shape[1]
     local_experts = gate_up.shape[0]
     ff_local = gate_up.shape[3]
     capacity = min(seq_count, max(2, 8 * seq_count * top_count // (3 * experts)))
-    expert_iota = jnp.arange(experts, dtype=jnp.int32)
-    nz_ny = 2 ** (int(math.log2(dp_count)) // 2)
-    if capacity >= seq_count and local_experts == 1 and nz_ny == 2 and tp_count == 2 * CORES:
-        wide = pad_up(col_count, 256)
-        first = col_count - (wide - LANE) + 1
-        lane_iota = jnp.arange(LANE, dtype=jnp.int32) - first
-        chosen_lanes = jnp.any(expert_ids[:, :, None] == lane_iota[None, None, :], axis=1).astype(jnp.float32)
-        return moe(
-            residual, moe_slice, router.T.astype(jnp.float32), chosen_lanes,
-            jnp.transpose(gate_up[0], (1, 2, 0)), w_down[0].T, dp_count, nz_ny, tp_count, 1)
     moe_sq = jnp.sum(residual * residual, axis=1)
     router_wide = router.astype(jnp.float32)
     gained = residual * moe_slice[None, :]
@@ -761,6 +997,7 @@
     moe_scale = lax.rsqrt(stats[:, :1] / full_width + norm_eps)
     logits = stats[:, 1:] * moe_scale
     hidden_rows = (gained * moe_scale).astype(jnp.bfloat16)
+    expert_iota = jnp.arange(experts, dtype=jnp.int32)
     chosen = expert_ids[:, :, None] == expert_iota[None, None, :]
     picked = jnp.sum(jnp.where(chosen, logits[:, None, :], 0.0), axis=-1)
     raised_logits = jnp.exp(picked)

time: 148 us -> 112 us (0.76)
  the two profiles are of different devices: /device:TPU:0 before, /device:TPU:28 now
where the time goes in v2:
time: 112 us
  Pallas kernels  108 us (96%)
  local copies, waits for them, and re-layouts  4.32 us (4%)
    pallas_call x1, Pallas kernels, moe(): pl.pallas_call(functools.partial(moe_kernel, dp, ny, tp, experts), out_sh...  84.7 us
    pallas_call x1, Pallas kernels, attend_block(): pl.pallas_call(functools.partial(attend_kernel, tp, kv_heads, heads // kv...  23 us

profile of v2, /device:TPU:28, one launch (start us, length us, event | category | flops | bytes accessed | tf_op | source)
XLA Modules:
  0.0 112.1 jit_solution(15820017836843658570)
XLA Ops:
  0.0 1.3 %broadcast_in_dim.15.gain_ref = f32[1,2880]{1,0:T(1,128)} reshape(f32[2880]{0:T(1024)} %param.15) | data formatting | bytes 23040 | tf_op jit(solution)/shard_map/broadcast_in_dim | solution.py:886
  1.3 1.3 %broadcast_in_dim.19.gain_ref = f32[1,2880]{1,0:T(1,128)} reshape(f32[2880]{0:T(1024)} %param.22) | data formatting | bytes 23040 | tf_op jit(solution)/shard_map/broadcast_in_dim | solution.py:659
  2.6 23.0 %shard_map.136.res_ref = f32[96,768]{1,0:T(8,128)} custom-call(bf16[96,720]{1,0:T(8,128)(2,1)} %tok_ref.1, f32[1,2880]{1,0:T(1,128)} %broadcast_in_dim.15.gain_ref, f32[1,128]{1,0:T(1,128)} %constant.7.inverse_ref, s32[1,96]{1,0:T(1,128)} %bitcast.14, f32[1,8]{1,0:T(1,128)} %bitcast.15, bf16[2880,512]{1,0:T(8,128)(2,1)} %wq_hbm.1, ...), custom_call_target="tpu_custom_call" | custom-call | flops 849346560 | bytes 11796480 | tf_op jit(solution)/shard_map/pallas_call | solution.py:860
  25.7 84.7 %shard_map.137 = f32[96,720]{1,0:T(8,128)} custom-call(f32[96,768]{1,0:T(8,128)} %shard_map.136.res_ref, f32[1,2880]{1,0:T(1,128)} %broadcast_in_dim.19.gain_ref, bf16[8,720]{1,0:T(8,128)(2,1)} %bitcast.18, s32[4,96]{1,0:T(4,128)} %bitcast.19, bf16[2,720,2880]{2,1,0:T(8,128)(2,1)} %bitcast.16, bf16[720,2880]{1,0:T(8,128)(2,1)} %bitcast.17), custom_call_target="tpu_custom_call" | custom-call | flops 9555148800 | bytes 12441600 | tf_op jit(solution)/shard_map/pallas_call | solution.py:639
  110.4 1.7 %copy.16 = f32[96,720]{1,0:T(8,128)} copy(f32[96,720]{1,0:T(8,128)} %shard_map.137) | data formatting | bytes 552960

commit v3 on v0

--- a/solution.py
+++ b/solution.py
@@ -3,6 +3,7 @@
 
 import jax
 import jax.numpy as jnp
+import numpy as np
 from jax import lax
 from jax.experimental import pallas as pl
 from jax.experimental.pallas import tpu as pltpu
@@ -348,6 +349,566 @@
     )(x)
 
 
+LANE = 128
+
+
+def pad_up(n, m):
+    return -(-n // m) * m
+
+
+def dot_t(a, b):
+    return lax.dot_general(a, b, (((1,), (1,)), ((), ())), preferred_element_type=jnp.float32)
+
+
+def widen(tp, cols, wide, raw, padded, lead):
+    block = 48
+    blocks = raw.shape[-2] // block
+
+    def body(i, carry):
+        at = pl.ds(pl.multiple_of(i * block, 16), block)
+        v = raw[lead + (at, slice(None))]
+        for t in range(tp):
+            part = v[:, t * cols:(t + 1) * cols]
+            padded[lead + (at, pl.ds(t * wide, wide))] = jnp.concatenate(
+                [part, jnp.zeros((block, wide - cols), v.dtype)], axis=1)
+        return carry
+    lax.fori_loop(0, blocks, body, 0)
+    rest = padded.shape[-2] - raw.shape[-2]
+    padded[lead + (pl.ds(raw.shape[-2], rest), slice(None))] = jnp.zeros((rest, tp * wide), padded.dtype)
+
+
+def attend_part(
+    tp, kv_heads, group_size, head_size, meet, meanwhile, res_buf,
+    tok_ref, gain_ref, inverse_ref, pos_ref, sink_ref, wq_hbm, wkv_hbm, wo_hbm, cache_hbm,
+    tok_buf, wq_buf, wkv_raw, wkv_wide, wkv_buf, wo_buf, cache_buf, q_rows, new_rows, pos_rows, att_rows,
+    part_buf, got_buf, load_sem, send_sem, recv_tok, recv_part,
+):
+    dp_id = lax.axis_index("dp")
+    me = lax.axis_index("tp")
+    core, chip = lax.rem(me, CORES), me // CORES
+    seq, cols = tok_ref.shape
+    wide = res_buf.shape[1]
+    window = cache_hbm.shape[2]
+    heads = kv_heads * group_size
+    twin_t = chip * CORES + 1 - core
+    across_t = (1 - chip) * CORES + core
+    corner_t = (1 - chip) * CORES + 1 - core
+    twin, across = (dp_id, twin_t), (dp_id, across_t)
+
+    loads = [
+        pltpu.make_async_copy(src, dst, load_sem.at[i]) for i, (src, dst) in enumerate(
+            [(wkv_hbm, wkv_raw), (wq_hbm, wq_buf), (cache_hbm, cache_buf), (wo_hbm, wo_buf)])
+    ]
+    for load in loads:
+        load.start()
+    own = pltpu.make_async_copy(tok_ref, tok_buf.at[me], load_sem.at[4])
+    own.start()
+    meet()
+
+    def token_copy(src, t, i, target):
+        return pltpu.make_async_remote_copy(
+            src_ref=src, dst_ref=tok_buf.at[t], send_sem=send_sem.at[i], recv_sem=recv_tok.at[t],
+            device_id=target, device_id_type=MESH)
+
+    def token_arrived(t):
+        token_copy(tok_buf.at[t], t, 0, twin).wait_recv()
+
+    sent = [token_copy(tok_ref, me, 0, across), token_copy(tok_ref, me, 1, twin)]
+    for copy in sent:
+        copy.start()
+
+    lanes = lax.broadcasted_iota(jnp.int32, (seq, LANE), 1)
+
+    def column(row):
+        n = row.shape[1]
+        square = lax.broadcasted_iota(jnp.int32, (n, n), 0) == lax.broadcasted_iota(jnp.int32, (n, n), 1)
+        return jnp.sum(jnp.where(square, row, 0.0), axis=1, keepdims=True)
+
+    position = jnp.broadcast_to(column(pos_ref[...].astype(jnp.float32)), (seq, LANE))
+    angles = position * inverse_ref[...]
+    cosine = jnp.cos(angles)
+    front = lax.rem(lanes, head_size) < head_size // 2
+    sine = jnp.where(front, -jnp.sin(angles), jnp.sin(angles))
+    for h in range(heads):
+        pos_rows[pl.ds(h, seq, stride=heads), :] = position
+    sink = jnp.broadcast_to(column(sink_ref[...]), (heads, LANE))
+    sink = jnp.concatenate([sink] * 8, axis=0)
+
+    loads[0].wait()
+    kv_rows = wkv_raw.shape[0]
+    step = kv_rows // 30
+
+    def split(i, carry):
+        at = pl.multiple_of(i * step, 16)
+        wkv_wide[...] = wkv_raw[pl.ds(at, step), :].astype(jnp.float32)
+        half = pl.ds(pl.multiple_of(i * (step // kv_heads), 16), step // kv_heads)
+        for h in range(kv_heads):
+            wkv_buf[half, h * LANE:(h + 1) * LANE] = wkv_wide[
+                pl.ds(h, step // kv_heads, stride=kv_heads), :].astype(jnp.bfloat16)
+        return carry
+    lax.fori_loop(0, 30, split, 0)
+
+    token_arrived(across_t)
+    forward = token_copy(tok_buf.at[across_t], across_t, 2, twin)
+    forward.start()
+    sent.append(forward)
+    own.wait()
+    token_arrived(twin_t)
+    token_arrived(corner_t)
+    loads[1].wait()
+
+    pieces = [tok_buf[t].astype(jnp.float32) for t in range(tp)]
+    squares = jnp.sum(pieces[0] * pieces[0], axis=1, keepdims=True)
+    for v in pieces[1:]:
+        squares = squares + jnp.sum(v * v, axis=1, keepdims=True)
+    scale = lax.rsqrt(squares / (tp * cols) + norm_eps)
+    gains = gain_ref[...].reshape(1, tp * cols)
+    queries, fresh = 0.0, 0.0
+    for t in range(tp):
+        at = slice(t * cols, (t + 1) * cols)
+        normed = (pieces[t] * scale * gains[:, at]).astype(jnp.bfloat16)
+        queries = queries + jnp.dot(normed, wq_buf[at, :], preferred_element_type=jnp.float32)
+        fresh = fresh + jnp.dot(normed, wkv_buf[at, :], preferred_element_type=jnp.float32)
+
+    def turned(v):
+        swapped = jnp.where(
+            front, pltpu.roll(v, LANE - head_size // 2, 1), pltpu.roll(v, head_size // 2, 1))
+        return v * cosine + swapped * sine
+
+    def rounded(v):
+        return v.astype(jnp.bfloat16).astype(jnp.float32)
+
+    low = lanes < head_size
+    for h in range(heads):
+        if h % 2 == 0:
+            pair = rounded(turned(queries[:, h // 2 * LANE:(h // 2 + 1) * LANE]))
+        if h % group_size == 0:
+            k = h // group_size
+            entry = fresh[:, k * LANE:(k + 1) * LANE]
+            entry = rounded(jnp.where(low, turned(entry), entry))
+        own_q = pair if h % 2 == 0 else pltpu.roll(pair, head_size, 1)
+        q_rows[pl.ds(h, seq, stride=heads), :] = jnp.where(low, own_q, 0.0)
+        new_rows[pl.ds(h, seq, stride=heads), :] = entry
+
+    loads[2].wait()
+    batch = 8
+    rows = batch * heads
+    slot = lax.broadcasted_iota(jnp.int32, (rows, LANE), 1)
+    upper = lax.broadcasted_iota(jnp.int32, (heads, LANE), 0) < group_size
+    score_scale = head_size ** (-0.5)
+
+    def attend(i, carry):
+        at = pl.ds(pl.multiple_of(i * rows, rows), rows)
+        q = q_rows[at, :]
+        entry = new_rows[at, :]
+        pos = pos_rows[at, :].astype(jnp.int32)
+        raw = []
+        for s in range(batch):
+            qs = q[s * heads:(s + 1) * heads]
+            lhs = jnp.concatenate(
+                [jnp.where(upper, qs, 0.0), jnp.where(upper, 0.0, qs)], axis=1).astype(jnp.bfloat16)
+            rhs = jnp.concatenate([cache_buf[i * batch + s, k] for k in range(kv_heads)], axis=1)
+            raw.append(dot_t(lhs, rhs))
+        scores = jnp.concatenate(raw, axis=0) * score_scale
+        fresh_score = jnp.sum(q * entry, axis=1, keepdims=True) * score_scale
+        current = slot == lax.rem(pos, window)
+        scores = jnp.where(current, fresh_score, jnp.where(slot <= pos, scores, -jnp.inf))
+        peak = jnp.maximum(jnp.max(scores, axis=1, keepdims=True), sink)
+        raised = jnp.exp(scores - peak)
+        denominator = jnp.sum(raised, axis=1, keepdims=True) + jnp.exp(sink - peak)
+        probs = rounded(raised / denominator)
+        fresh_prob = jnp.sum(jnp.where(current, probs, 0.0), axis=1, keepdims=True)
+        probs = jnp.where(current, 0.0, probs)
+        mixed = []
+        for s in range(batch):
+            lhs = probs[s * heads:(s + 1) * heads].astype(jnp.bfloat16)
+            rhs = jnp.concatenate([cache_buf[i * batch + s, k] for k in range(kv_heads)], axis=1)
+            both = jnp.dot(lhs, rhs, preferred_element_type=jnp.float32)
+            mixed.append(jnp.where(upper, both[:, :LANE], both[:, LANE:]))
+        att_rows[at, :] = jnp.concatenate(mixed, axis=0) + fresh_prob * entry
+        return carry
+
+    lax.fori_loop(0, seq // batch, attend, 0)
+
+    tiles = []
+    for j in range(heads // 2):
+        even = att_rows[pl.ds(2 * j, seq, stride=heads), :]
+        odd = att_rows[pl.ds(2 * j + 1, seq, stride=heads), :]
+        tiles.append(jnp.where(low, pltpu.roll(even, head_size, 1), odd).astype(jnp.bfloat16))
+    attended = jnp.concatenate(tiles, axis=1)
+    loads[3].wait()
+
+    def share(t):
+        return dot_t(attended, wo_buf[pl.ds(pl.multiple_of(t * cols, 16), cols), :])
+
+    def part_copy(i, target):
+        return pltpu.make_async_remote_copy(
+            src_ref=part_buf.at[i], dst_ref=got_buf.at[i], send_sem=send_sem.at[3 + i],
+            recv_sem=recv_part.at[i], device_id=target, device_id_type=MESH)
+
+    parts = [part_copy(0, twin), part_copy(1, across), part_copy(2, twin)]
+    part_buf[0] = share(corner_t).astype(jnp.bfloat16)
+    parts[0].start()
+    far = share(across_t)
+    parts[0].wait_recv()
+    part_buf[1] = (far + got_buf[0].astype(jnp.float32)).astype(jnp.bfloat16)
+    parts[1].start()
+    part_buf[2] = share(twin_t).astype(jnp.bfloat16)
+    parts[2].start()
+    total = tok_ref[...].astype(jnp.float32) + share(me)
+    meanwhile()
+    parts[2].wait_recv()
+    total = total + got_buf[2].astype(jnp.float32)
+    parts[1].wait_recv()
+    total = total + got_buf[1].astype(jnp.float32)
+    res_buf[...] = jnp.concatenate([total, jnp.zeros((seq, wide - cols), jnp.float32)], axis=1)
+    for copy in sent + parts:
+        copy.wait_send()
+
+
+def moe_part(
+    dp, ny, tp, experts, cuts, full,
+    res_ref, gain_ref, router_ref, ids_ref, wd_load, out_ref,
+    rows_buf, gu_pad, wd_raw, wd_pad, act_buf, out_buf, back_buf,
+    s_twin, s_x, s_y, s_z, r_rows, s_act, r_act, s_out, r_out,
+):
+    nz = dp // ny
+    dp_id = lax.axis_index("dp")
+    me = lax.axis_index("tp")
+    core, chip = lax.rem(me, CORES), me // CORES
+    z, y = dp_id // ny, lax.rem(dp_id, ny)
+    seq, wide = res_ref.shape
+    cols = out_ref.shape[1]
+    twin_t = chip * CORES + 1 - core
+    across_t = (1 - chip) * CORES + core
+    corner_t = (1 - chip) * CORES + 1 - core
+    twin, across = (dp_id, twin_t), (dp_id, across_t)
+    y_peer = (z * ny + 1 - y, me)
+
+    res = res_ref[...]
+    gains = gain_ref[...].reshape(1, full)
+    gain = gains[:, :cols]
+    for t in range(1, tp):
+        gain = jnp.where(me == t, gains[:, t * cols:(t + 1) * cols], gain)
+    gained = res * jnp.concatenate([gain, jnp.zeros((1, wide - cols), jnp.float32)], axis=1)
+    values = [jnp.sum(res * res, axis=1, keepdims=True)]
+    router = jnp.concatenate(
+        [router_ref[...].astype(jnp.float32), jnp.zeros((experts, wide - cols), jnp.float32)], axis=1)
+    for e in range(experts):
+        values.append(jnp.sum(gained * router[e:e + 1, :], axis=1, keepdims=True))
+    tail = cols - (wide - LANE)
+    lanes = lax.broadcasted_iota(jnp.int32, (seq, LANE), 1)
+    group = (LANE - tail) // 3
+    spread = jnp.zeros((seq, LANE), jnp.float32)
+    for j, v in enumerate(values):
+        for g in range(3):
+            spread = jnp.where(lanes == tail + g * group + j, v, spread)
+    high = spread.astype(jnp.bfloat16).astype(jnp.float32)
+    middle = (spread - high).astype(jnp.bfloat16).astype(jnp.float32)
+    low = spread - high - middle
+    last = jnp.where(lanes < tail, gained[:, wide - LANE:], jnp.where(
+        lanes < tail + group, high, jnp.where(lanes < tail + 2 * group, middle, low)))
+    rows_buf[dp_id, me, :, :wide - LANE] = gained[:, :wide - LANE].astype(jnp.bfloat16)
+    rows_buf[dp_id, me, :, wide - LANE:] = last.astype(jnp.bfloat16)
+
+    share = seq // cuts
+
+    def piece(b, t, h, sem, target):
+        view = rows_buf.at[b, t, pl.ds(h * share, share)]
+        return pltpu.make_async_remote_copy(
+            src_ref=view, dst_ref=view, send_sem=sem, recv_sem=r_rows.at[b, t, h],
+            device_id=target, device_id_type=MESH)
+
+    def to_twin(b, t, h):
+        return piece(b, t, h, s_twin.at[b, t, h], twin)
+
+    def to_x(p, h):
+        return piece(p * ny + y, me, h, s_x.at[p, h], across)
+
+    def to_y(b, t, h):
+        return piece(b, t, h, s_y.at[b, t // CORES, h], y_peer)
+
+    def to_z(p, h):
+        return piece(dp_id, me, h, s_z.at[p, h], (p * ny + y, me))
+
+    def arrived(b, t, h):
+        piece(b, t, h, r_rows.at[b, t, h], twin).wait_recv()
+
+    def plane(k):
+        return jnp.where(2 * z < nz, lax.rem(z + k, nz), lax.rem(z - k + nz, nz))
+
+    for h in range(cuts):
+        to_x(z, h).start()
+        to_y(dp_id, me, h).start()
+        to_twin(dp_id, me, h).start()
+
+    def send_far(k, carry):
+        for h in range(cuts):
+            to_z(plane(k), h).start()
+        return carry
+    lax.fori_loop(1, nz, send_far, 0)
+
+    def column_in(k, y_too):
+        p = plane(k)
+        for h in range(cuts):
+            arrived(p * ny + y, me, h)
+            to_x(p, h).start()
+            if y_too:
+                to_y(p * ny + y, me, h).start()
+            to_twin(p * ny + y, me, h).start()
+
+    def column_to_y(k):
+        for h in range(cuts):
+            to_y(plane(k) * ny + y, me, h).start()
+
+    def across_in(k):
+        b = plane(k) * ny + y
+        for h in range(cuts):
+            arrived(b, across_t, h)
+            to_y(b, across_t, h).start()
+            to_twin(b, across_t, h).start()
+
+    column_in(1, True)
+    for k in range(2, nz):
+        column_in(k, False)
+        across_in(k - 1)
+        if k == 2:
+            across_in(0)
+        column_to_y(k)
+        if k == 2:
+            wd_load.wait()
+            widen(tp, cols, wide, wd_raw, wd_pad, ())
+
+    tile_n = 256
+    n_tiles = wide // tile_n
+
+    def act_copy(t, p, n, i, target):
+        view = act_buf.at[t, p, n]
+        return pltpu.make_async_remote_copy(
+            src_ref=view, dst_ref=view, send_sem=s_act.at[i, p, n], recv_sem=r_act.at[t, p, n],
+            device_id=target, device_id_type=MESH)
+
+    def act_arrived(t, p, n):
+        act_copy(t, p, n, 0, twin).wait_recv()
+
+    def out_copy(b, n):
+        return pltpu.make_async_remote_copy(
+            src_ref=out_buf.at[b, n], dst_ref=back_buf.at[dp_id, n], send_sem=s_out.at[b, n],
+            recv_sem=r_out.at[dp_id, n], device_id=(b, me), device_id_type=MESH)
+
+    def stats_tile(b):
+        total = rows_buf[b, 0, :, wide - LANE:].astype(jnp.float32)
+        for t in range(1, tp):
+            total = total + rows_buf[b, t, :, wide - LANE:].astype(jnp.float32)
+        total = jnp.where(lanes >= tail, total, 0.0)
+        return total
+
+    def row_scale(total):
+        hit = (lanes == tail) | (lanes == tail + group) | (lanes == tail + 2 * group)
+        squares = jnp.sum(jnp.where(hit, total, 0.0), axis=1, keepdims=True)
+        return lax.rsqrt(squares / full + norm_eps)
+
+    def up_project(p):
+        scale = jnp.concatenate([row_scale(stats_tile(p * ny + b)) for b in range(ny)], axis=0)
+
+        def body(n, carry):
+            at = pl.ds(pl.multiple_of(n * tile_n, tile_n), tile_n)
+            lhs = jnp.concatenate([
+                jnp.concatenate([rows_buf[p * ny + b, t] for t in range(tp)], axis=1)
+                for b in range(ny)], axis=0)
+            gate = dot_t(lhs, gu_pad[0, at, :]) * scale
+            up = dot_t(lhs, gu_pad[1, at, :]) * scale
+            act_buf[me, p, n] = (gate * jax.nn.sigmoid(glu_alpha * gate) * (up + 1.0)).astype(jnp.bfloat16)
+            act_copy(me, p, n, 0, across).start()
+            act_copy(me, p, n, 1, twin).start()
+            return carry
+        lax.fori_loop(0, n_tiles, body, 0)
+
+    def down_project(p):
+        def body(n, carry):
+            at = pl.ds(pl.multiple_of(n * tile_n, tile_n), tile_n)
+            lhs = jnp.concatenate([act_buf[t, p, i] for t in range(tp) for i in range(n_tiles)], axis=1)
+            out = dot_t(lhs, wd_pad[at, :]).astype(jnp.bfloat16)
+            for b in range(ny):
+                out_buf[p * ny + b, n] = out[b * seq:(b + 1) * seq]
+            for b in range(ny):
+                @pl.when(p * ny + b != dp_id)
+                def _():
+                    out_copy(p * ny + b, n).start()
+
+                @pl.when(p * ny + b == dp_id)
+                def _():
+                    back_buf[dp_id, n] = out[b * seq:(b + 1) * seq]
+            return carry
+        lax.fori_loop(0, n_tiles, body, 0)
+
+    def stage(k, carry):
+        @pl.when(k < nz)
+        def _():
+            p = plane(k + 1)
+            for t in (me, across_t):
+                b = p * ny + 1 - y
+                for h in range(cuts):
+                    arrived(b, t, h)
+                    to_twin(b, t, h).start()
+            for b in range(ny):
+                for t in (twin_t, corner_t):
+                    for h in range(cuts):
+                        arrived(p * ny + b, t, h)
+            up_project(p)
+
+        @pl.when(k == 0)
+        def _():
+            across_in(nz - 1)
+
+        @pl.when(k > 0)
+        def _():
+            p = plane(k)
+            for n in range(n_tiles):
+                act_arrived(across_t, p, n)
+                act_copy(across_t, p, n, 2, twin).start()
+            for n in range(n_tiles):
+                act_arrived(twin_t, p, n)
+                act_arrived(corner_t, p, n)
+            down_project(p)
+        return carry
+
+    lax.fori_loop(0, nz + 1, stage, 0)
+
+    total = stats_tile(dp_id)
+    scale = row_scale(total)
+    shift = LANE - group
+    summed = total + pltpu.roll(total, shift, 1) + pltpu.roll(pltpu.roll(total, shift, 1), shift, 1)
+    square = lax.broadcasted_iota(jnp.int32, (seq, seq), 0) == lax.broadcasted_iota(jnp.int32, (seq, seq), 1)
+    chosen = lanes < 0
+    for k in range(ids_ref.shape[0]):
+        named = ids_ref[k:k + 1, :].astype(jnp.float32)
+        named = jnp.sum(jnp.where(square, named, 0.0), axis=1, keepdims=True).astype(jnp.int32)
+        chosen = chosen | (lanes == named + tail + 1)
+    raised = jnp.where(chosen, jnp.exp(jnp.where(chosen, summed * scale, 0.0)), 0.0)
+    weights = raised / jnp.sum(raised, axis=1, keepdims=True)
+
+    def wait_out(d, carry):
+        b = lax.rem(dp_id + d, dp)
+        for n in range(n_tiles):
+            view = back_buf.at[b, n]
+            pltpu.make_async_remote_copy(
+                src_ref=view, dst_ref=view, send_sem=r_out.at[b, n], recv_sem=r_out.at[b, n],
+                device_id=twin, device_id_type=MESH).wait_recv()
+        return carry
+
+    lax.fori_loop(1, dp, wait_out, 0)
+    parts = []
+    for n in range(n_tiles):
+        part = res[:, n * tile_n:(n + 1) * tile_n]
+        for e in range(dp):
+            part = part + weights[:, tail + 1 + e:tail + 2 + e] * back_buf[e, n].astype(jnp.float32)
+        parts.append(part)
+    out_ref[...] = jnp.concatenate(parts, axis=1)[:, :cols]
+
+    def drain(p, carry):
+        for h in range(cuts):
+            to_x(p, h).wait_send()
+
+            @pl.when(p != z)
+            def _():
+                to_z(p, h).wait_send()
+            for t in (me, across_t):
+                to_y(p * ny + y, t, h).wait_send()
+                for b in range(ny):
+                    to_twin(p * ny + b, t, h).wait_send()
+        return carry
+    lax.fori_loop(0, nz, drain, 0)
+    def drain_acts(p, carry):
+        for n in range(n_tiles):
+            act_copy(me, p, n, 0, across).wait_send()
+            act_copy(me, p, n, 1, twin).wait_send()
+            act_copy(across_t, p, n, 2, twin).wait_send()
+        return carry
+    lax.fori_loop(0, nz, drain_acts, 0)
+
+    def drain_outs(d, carry):
+        for n in range(n_tiles):
+            out_copy(lax.rem(dp_id + d, dp), n).wait_send()
+        return carry
+    lax.fori_loop(1, dp, drain_outs, 0)
+
+
+def layer_kernel(
+    dp, ny, tp, experts, cuts, kv_heads, group_size, head_size,
+    tok_ref, gain_ref, inverse_ref, pos_ref, sink_ref, moe_gain_ref, router_ref, ids_ref,
+    wq_hbm, wkv_hbm, wo_hbm, cache_hbm, gu_hbm, wd_hbm, out_ref, *scratch,
+):
+    res_buf, gu_raw, wd_raw, load_sem = scratch[:4]
+    attend_scratch, (rows_buf, gu_pad, wd_pad, *rest) = scratch[4:21], scratch[21:]
+    dp_id, me = lax.axis_index("dp"), lax.axis_index("tp")
+    core, chip = lax.rem(me, CORES), me // CORES
+    cols, full = gu_hbm.shape[1:]
+    wide = res_buf.shape[1]
+    gu_load = pltpu.make_async_copy(gu_hbm, gu_raw, load_sem.at[0])
+    wd_load = pltpu.make_async_copy(wd_hbm, wd_raw, load_sem.at[1])
+
+    def meet():
+        gu_load.start()
+        wd_load.start()
+        near = [(dp_id, chip * CORES + 1 - core), (dp_id, (1 - chip) * CORES + core)]
+        greet(near + [(lax.rem(dp_id + d, dp), me) for d in range(1, dp)])
+
+    def meanwhile():
+        gu_load.wait()
+        for half in range(2):
+            widen(tp, cols, wide, gu_raw, gu_pad, (half,))
+
+    attend_part(
+        tp, kv_heads, group_size, head_size, meet, meanwhile, res_buf,
+        tok_ref, gain_ref, inverse_ref, pos_ref, sink_ref, wq_hbm, wkv_hbm, wo_hbm, cache_hbm, *attend_scratch)
+    moe_part(
+        dp, ny, tp, experts, cuts, full, res_buf, moe_gain_ref, router_ref, ids_ref, wd_load, out_ref,
+        rows_buf, gu_pad, wd_raw, wd_pad, *rest)
+
+
+def layer(tokens, gain, positions, sinks, moe_gain, router, ids, w_query, w_keyvalue, w_out, cache, gate_up, w_down, dp, ny, tp):
+    seq, cols = tokens.shape
+    wide = pad_up(cols, 256)
+    full = tp * cols
+    kv_heads, window, entry = cache.shape[1:]
+    head_size = entry // 2
+    heads = w_query.shape[1] // head_size
+    exponent = np.arange(LANE) % (head_size // 2) * (2.0 / head_size)
+    inverse = jnp.asarray(rope_base ** -exponent, jnp.float32)[None, :]
+    nz, cuts, tiles = dp // ny, 2, wide // 256
+    bf, f32 = jnp.bfloat16, jnp.float32
+    dma, vmem = pltpu.SemaphoreType.DMA, pltpu.VMEM
+    return pl.pallas_call(
+        functools.partial(
+            layer_kernel, dp, ny, tp, router.shape[0], cuts, kv_heads, heads // kv_heads, head_size),
+        out_shape=jax.ShapeDtypeStruct((seq, cols), f32),
+        in_specs=[pl.BlockSpec(memory_space=pltpu.VMEM)] * 8 + [pl.BlockSpec(memory_space=pl.ANY)] * 6,
+        out_specs=pl.BlockSpec(memory_space=pltpu.VMEM),
+        scratch_shapes=[
+            vmem((seq, wide), f32), vmem((2, cols, full), bf), vmem((cols, full), bf), dma((2,)),
+            vmem((tp, seq, cols), bf), vmem(w_query.shape, bf), vmem((full * kv_heads, LANE), bf),
+            vmem((full * kv_heads // 30, LANE), f32), vmem((full, kv_heads * LANE), bf),
+            vmem((full, heads * head_size), bf), vmem(cache.shape, bf),
+            vmem((seq * heads, LANE), f32), vmem((seq * heads, LANE), f32),
+            vmem((seq * heads, LANE), f32), vmem((seq * heads, LANE), f32),
+            vmem((3, seq, cols), bf), vmem((3, seq, cols), bf),
+            dma((5,)), dma((6,)), dma((tp,)), dma((3,)),
+            vmem((dp, tp, seq, wide), bf), vmem((2, wide, tp * wide), bf), vmem((wide, tp * wide), bf),
+            vmem((tp, nz, tiles, ny * seq, 256), bf),
+            vmem((dp, tiles, seq, 256), bf), vmem((dp, tiles, seq, 256), bf),
+            dma((dp, tp, cuts)), dma((nz, cuts)), dma((dp, tp // CORES, cuts)),
+            dma((nz, cuts)), dma((dp, tp, cuts)),
+            dma((3, nz, tiles)), dma((tp, nz, tiles)), dma((dp, tiles)), dma((dp, tiles)),
+        ],
+        compiler_params=pltpu.CompilerParams(
+            collective_id=0, has_side_effects=True, vmem_limit_bytes=67_000_000),
+        cost_estimate=pl.CostEstimate(
+            flops=6 * dp * seq * full * cols, bytes_accessed=6 * full * cols, transcendentals=0),
+    )(tokens, gain, inverse, positions[None, :], sinks[None, :], moe_gain, router, ids,
+      w_query, w_keyvalue.reshape(full * kv_heads, LANE), w_out.T, cache, gate_up, w_down)
+
+
 def activate(mixed_in, ff_local):
     gate_part = mixed_in[..., :ff_local]
     up_part = mixed_in[..., ff_local:]
@@ -381,6 +942,12 @@
     q_local = w_query.shape[1] // head_size
     group_size = q_local // kv_local
     window = window_cache.shape[2]
+    ny = 2 ** (int(math.log2(dp_count)) // 2)
+    if (tp_count, ny, gate_up.shape[0], kv_local, group_size, window, 2 * head_size) == (
+            2 * CORES, 2, 1, 2, 4, LANE, LANE) and dp_count > 2 * ny:
+        return layer(
+            tokens, attn_gain, positions, attn_sinks, moe_gain, router.T, expert_ids.T, w_query, w_keyvalue,
+            w_out, window_cache, jnp.transpose(gate_up[0], (1, 2, 0)), w_down[0].T, dp_count, ny, tp_count)
     moe_slice = lax.dynamic_slice_in_dim(moe_gain, col_start, col_count)
     tok_wide = tokens.astype(jnp.float32)
     kv_flat = w_keyvalue.reshape(full_width, kv_local * 2 * head_size)

time: 193 us -> 98.8 us (0.51)
  matrix products: 41.4 us -> 0 us
  local copies, waits for them, and re-layouts: 24 us -> 1.69 us
  waiting for transfers between devices: 15.2 us -> 0 us
  other arithmetic: 12.9 us -> 0 us
  starting transfers between devices: 10.4 us -> 0 us
  Pallas kernels: 87.2 us -> 96.9 us
    dot_general x9 -> x0, matrix products: 41.4 us -> none  [the longest x2 10.9 us: on_device(): out = jnp.dot(act_all, w_down[e], preferred_element_type=jnp.float32)]
    all_to_all x2 -> x0, waiting for transfers between devices: 15.2 us -> none  [on_device(): lax.all_to_all(jnp.stack(outs, axis=1), 'dp', split_axis=0, concat_axis=0...]
    all_to_all x2 -> x0, starting transfers between devices: 10.4 us -> none  [on_device(): lax.all_to_all(jnp.stack(outs, axis=1), 'dp', split_axis=0, concat_axis=0...]
    pallas_call x6 -> x1, Pallas kernels: 87.2 us -> 96.9 us  [layer(): pl.pallas_call(functools.partial(layer_kernel, dp, ny, tp, router.shape[0...]
    convert_element_type x4 -> x0, local copies, waits for them, and re-layouts: 6.18 us -> none  [the longest x2 4.29 us: on_device(): outs.append(out.astype(jnp.bfloat16).reshape(dp_count, half, col_count))]
    dot_general x1 -> x0, local copies, waits for them, and re-layouts: 4.92 us -> none  [on_device(): jnp.dot(piece_rows, kv_flat, preferred_element_type=jnp.float32)]
    another operation x2 -> x0, local copies, waits for them, and re-layouts: 3.32 us -> none
    convert_element_type x5 -> x0, other arithmetic: 3.07 us -> none  [the longest x1 1.36 us: on_device(): (raised_new / denominator).astype(jnp.bfloat16).astype(jnp.float32)]
  transfers between devices with their start and end apart: 2 -> 0, of which waited for: 1 -> 0; matrix products, arithmetic and copies ran while one was open for 6% -> 0% of each run, Pallas kernels for 9% -> 0%
where the time goes in v3:
time: 98.8 us; the launch traced here: 98.6 us
  Pallas kernels  96.9 us (98%)
  local copies, waits for them, and re-layouts  1.69 us (2%)
    pallas_call x1, Pallas kernels, layer(): pl.pallas_call(functools.partial(layer_kernel, dp, ny, tp, router.shape[0...  96.9 us

profile of v3, /device:TPU:0, one launch (start us, length us, event | category | flops | bytes accessed | tf_op | source)
XLA Modules:
  0.0 98.6 jit_solution(17732988340493889397)
XLA Ops:
  0.0 96.9 %shard_map.136 = f32[96,720]{1,0:T(8,128)} custom-call(bf16[96,720]{1,0:T(8,128)(2,1)} %tok_ref.1, f32[2880]{0:T(1024)} %gain_ref.1, f32[1,128]{1,0:T(1,128)} %constant.7.inverse_ref, s32[1,96]{1,0:T(1,128)} %bitcast.18, f32[1,8]{1,0:T(1,128)} %bitcast.19, f32[2880]{0:T(1024)} %moe_gain_ref.1, bf16[8,720]{1,0:T(8,128)(2,1)} %bitcast.16, s32[4,96]{1,0:T(4,128)} %bitcast.17, ...), custom_call_target="tpu_custom_call" | custom-call | flops 9555148800 | bytes 12441600 | tf_op jit(solution)/shard_map/pallas_call | solution.py:882
  96.9 1.7 %copy.16 = f32[96,720]{1,0:T(8,128)} copy(f32[96,720]{1,0:T(8,128)} %shard_map.136) | data formatting | bytes 552960

commit v4 on v3

--- a/solution.py
+++ b/solution.py
@@ -448,27 +448,34 @@
         return carry
     lax.fori_loop(0, 30, split, 0)
 
+    gains = gain_ref[...].reshape(1, tp * cols)
+    loads[1].wait()
+
+    def project(t):
+        v = tok_buf[t].astype(jnp.float32)
+        gain = gains[:, :cols]
+        for i in range(1, tp):
+            gain = jnp.where(t == i, gains[:, i * cols:(i + 1) * cols], gain)
+        gained = (v * gain).astype(jnp.bfloat16)
+        at = pl.ds(pl.multiple_of(t * cols, 16), cols)
+        return (
+            jnp.sum(v * v, axis=1, keepdims=True),
+            jnp.dot(gained, wq_buf[at, :], preferred_element_type=jnp.float32),
+            jnp.dot(gained, wkv_buf[at, :], preferred_element_type=jnp.float32))
+
+    own.wait()
+    token_arrived(twin_t)
+    sums = [project(me), project(twin_t)]
     token_arrived(across_t)
     forward = token_copy(tok_buf.at[across_t], across_t, 2, twin)
     forward.start()
     sent.append(forward)
-    own.wait()
-    token_arrived(twin_t)
+    sums.append(project(across_t))
     token_arrived(corner_t)
-    loads[1].wait()
-
-    pieces = [tok_buf[t].astype(jnp.float32) for t in range(tp)]
-    squares = jnp.sum(pieces[0] * pieces[0], axis=1, keepdims=True)
-    for v in pieces[1:]:
-        squares = squares + jnp.sum(v * v, axis=1, keepdims=True)
+    sums.append(project(corner_t))
+    squares, queries, fresh = [a + b + c + d for a, b, c, d in zip(*sums)]
     scale = lax.rsqrt(squares / (tp * cols) + norm_eps)
-    gains = gain_ref[...].reshape(1, tp * cols)
-    queries, fresh = 0.0, 0.0
-    for t in range(tp):
-        at = slice(t * cols, (t + 1) * cols)
-        normed = (pieces[t] * scale * gains[:, at]).astype(jnp.bfloat16)
-        queries = queries + jnp.dot(normed, wq_buf[at, :], preferred_element_type=jnp.float32)
-        fresh = fresh + jnp.dot(normed, wkv_buf[at, :], preferred_element_type=jnp.float32)
+    queries, fresh = queries * scale, fresh * scale
 
     def turned(v):
         swapped = jnp.where(
@@ -788,23 +795,27 @@
     raised = jnp.where(chosen, jnp.exp(jnp.where(chosen, summed * scale, 0.0)), 0.0)
     weights = raised / jnp.sum(raised, axis=1, keepdims=True)
 
-    def wait_out(d, carry):
-        b = lax.rem(dp_id + d, dp)
+    out_ref[...] = res[:, :cols]
+
+    def add_back(b, fetch):
+        weight = jnp.sum(jnp.where(lanes == tail + 1 + b, weights, 0.0), axis=1, keepdims=True)
         for n in range(n_tiles):
-            view = back_buf.at[b, n]
-            pltpu.make_async_remote_copy(
-                src_ref=view, dst_ref=view, send_sem=r_out.at[b, n], recv_sem=r_out.at[b, n],
-                device_id=twin, device_id_type=MESH).wait_recv()
+            if fetch:
+                view = back_buf.at[b, n]
+                pltpu.make_async_remote_copy(
+                    src_ref=view, dst_ref=view, send_sem=r_out.at[b, n], recv_sem=r_out.at[b, n],
+                    device_id=twin, device_id_type=MESH).wait_recv()
+            used = min(tile_n, cols - n * tile_n)
+            at = slice(n * tile_n, n * tile_n + used)
+            out_ref[:, at] = out_ref[:, at] + weight * back_buf[b, n].astype(jnp.float32)[:, :used]
+
+    def add_far(i, carry):
+        add_back(plane(1 + i // ny) * ny + lax.rem(i, ny), True)
         return carry
 
-    lax.fori_loop(1, dp, wait_out, 0)
-    parts = []
-    for n in range(n_tiles):
-        part = res[:, n * tile_n:(n + 1) * tile_n]
-        for e in range(dp):
-            part = part + weights[:, tail + 1 + e:tail + 2 + e] * back_buf[e, n].astype(jnp.float32)
-        parts.append(part)
-    out_ref[...] = jnp.concatenate(parts, axis=1)[:, :cols]
+    add_back(dp_id, False)
+    lax.fori_loop(0, dp - ny, add_far, 0)
+    add_back(z * ny + 1 - y, True)
 
     def drain(p, carry):
         for h in range(cuts):

time: 98.8 us -> 98.3 us (level)
  no operation moved by 1% of the time
where the time goes in v4:
time: 98.3 us; the launch traced here: 98.1 us
  Pallas kernels  96.4 us (98%)
  local copies, waits for them, and re-layouts  1.69 us (2%)
    pallas_call x1, Pallas kernels, layer(): pl.pallas_call(functools.partial(layer_kernel, dp, ny, tp, router.shape[0...  96.4 us

profile of v4, /device:TPU:0, one launch (start us, length us, event | category | flops | bytes accessed | tf_op | source)
XLA Modules:
  0.0 98.1 jit_solution(8084502312626377977)
XLA Ops:
  0.0 96.4 %shard_map.136 = f32[96,720]{1,0:T(8,128)} custom-call(bf16[96,720]{1,0:T(8,128)(2,1)} %tok_ref.1, f32[2880]{0:T(1024)} %gain_ref.1, f32[1,128]{1,0:T(1,128)} %constant.7.inverse_ref, s32[1,96]{1,0:T(1,128)} %bitcast.18, f32[1,8]{1,0:T(1,128)} %bitcast.19, f32[2880]{0:T(1024)} %moe_gain_ref.1, bf16[8,720]{1,0:T(8,128)(2,1)} %bitcast.16, s32[4,96]{1,0:T(4,128)} %bitcast.17, ...), custom_call_target="tpu_custom_call" | custom-call | flops 9555148800 | bytes 12441600 | tf_op jit(solution)/shard_map/pallas_call | solution.py:893
  96.4 1.7 %copy.16 = f32[96,720]{1,0:T(8,128)} copy(f32[96,720]{1,0:T(8,128)} %shard_map.136) | data formatting | bytes 552960
